TPU v7x, 128 devices: a whole 4x4x4 slice. The times are simulated.
128 devices in a mesh: dp: 1, fsdp: 128 (over z, y, x, core).
Axes of the slice: x: 4, y: 4, z: 4, core: 2. Of those that a mesh axis runs over, the one named last changes fastest.
Arguments:
- prompts: bfloat16 [128, 512, 2304], P(('dp', 'fsdp'))
- ln1_gain: bfloat16 [2304], P('fsdp')
- ln1_bias: bfloat16 [2304], P('fsdp')
- w_qkv: bfloat16 [2304, 3, 24, 96], P('fsdp')
- b_qkv: bfloat16 [6912], P('fsdp')
- w_out: bfloat16 [2304, 2304], P('fsdp')
- b_out: bfloat16 [2304], P('fsdp')
- ln2_gain: bfloat16 [2304], P('fsdp')
- ln2_bias: bfloat16 [2304], P('fsdp')
- w_up: bfloat16 [2304, 9216], P('fsdp')
- b_up: bfloat16 [9216], P('fsdp')
- w_down: bfloat16 [9216, 2304], P('fsdp')
- b_down: bfloat16 [2304], P('fsdp')
Outputs:
- output 1: bfloat16 [128, 512, 2304], P(('dp', 'fsdp'))
- output 2: bfloat16 [128, 512, 24, 96], P(('dp', 'fsdp'))
- output 3: bfloat16 [128, 512, 24, 96], P(('dp', 'fsdp'))
All inputs are finite; a program needn't handle non-finite values.
Results may differ from a plain program's by a relative error of at most 0.00838182.
Values are sent between devices in bfloat16 or wider.
A program may use at most 1 GiB of HBM per device.

v0:
```python
import jax
import jax.numpy as jnp
from jax import lax
from jax.sharding import PartitionSpec as P

LN_EPS = 1e-5
QUERY_BLOCK = 256


def layer_norm(act, gain, shift):
    act_f32 = act.astype(jnp.float32)
    mean_val = jnp.mean(act_f32, axis=-1, keepdims=True)
    centered = act_f32 - mean_val
    var_val = jnp.mean(centered * centered, axis=-1, keepdims=True)
    normed = centered * lax.rsqrt(var_val + LN_EPS)
    return (normed * gain.astype(jnp.float32) + shift.astype(jnp.float32)).astype(jnp.bfloat16)


def causal_attention(queries, keys, values):
    seq_len = queries.shape[1]
    q_block = min(seq_len, QUERY_BLOCK)
    scale = queries.shape[-1] ** -0.5
    key_pos = jnp.arange(seq_len)

    def one_block(blk_idx):
        start = blk_idx * q_block
        q_blk = lax.dynamic_slice_in_dim(queries, start, q_block, axis=1)
        scores = jnp.einsum('bqhe,bkhe->bhqk', q_blk, keys, preferred_element_type=jnp.float32) * scale
        allowed = key_pos[None, :] <= (start + jnp.arange(q_block))[:, None]
        scores = jnp.where(allowed, scores, -jnp.inf)
        probs = jax.nn.softmax(scores, axis=-1).astype(jnp.bfloat16)
        return jnp.einsum('bhqk,bkhe->bqhe', probs, values, preferred_element_type=jnp.float32).astype(jnp.bfloat16)

    return lax.map(one_block, jnp.arange(seq_len // q_block))


def solution(mesh):
    batch_axes = ('dp', 'fsdp')

    def gather_full(shard):
        return lax.all_gather(shard, 'fsdp', axis=0, tiled=True)

    def local_layer(prompts, ln1_gain, ln1_bias, w_qkv, b_qkv, w_out, b_out, ln2_gain, ln2_bias, w_up, b_up, w_down, b_down):
        batch_loc, seq_len, d_model = prompts.shape
        heads, head_dim = w_qkv.shape[2], w_qkv.shape[3]
        normed1 = layer_norm(prompts, gather_full(ln1_gain), gather_full(ln1_bias))
        w_qkv_full = gather_full(w_qkv)
        b_qkv_full = gather_full(b_qkv)
        proj_qkv = jnp.einsum('bsd,djhe->jbshe', normed1, w_qkv_full, preferred_element_type=jnp.float32)
        proj_qkv = (proj_qkv + b_qkv_full.astype(jnp.float32).reshape(3, 1, 1, heads, head_dim)).astype(jnp.bfloat16)
        ctx_blocks = causal_attention(proj_qkv[0], proj_qkv[1], proj_qkv[2])
        w_out_full = gather_full(w_out).reshape(heads, head_dim, d_model)
        b_out_full = gather_full(b_out)
        attn_out = jnp.einsum('nbqhe,hec->bnqc', ctx_blocks, w_out_full, preferred_element_type=jnp.float32).reshape(batch_loc, seq_len, d_model)
        resid = (prompts.astype(jnp.float32) + attn_out + b_out_full.astype(jnp.float32)).astype(jnp.bfloat16)
        normed2 = layer_norm(resid, gather_full(ln2_gain), gather_full(ln2_bias))
        w_up_full = gather_full(w_up)
        b_up_full = gather_full(b_up)
        hidden = jnp.einsum('bsd,df->bsf', normed2, w_up_full, preferred_element_type=jnp.float32) + b_up_full.astype(jnp.float32)
        hidden = jax.nn.gelu(hidden, approximate=True).astype(jnp.bfloat16)
        w_down_full = gather_full(w_down)
        b_down_full = gather_full(b_down)
        mlp_out = jnp.einsum('bsf,fd->bsd', hidden, w_down_full, preferred_element_type=jnp.float32)
        layer_out = (resid.astype(jnp.float32) + mlp_out + b_down_full.astype(jnp.float32)).astype(jnp.bfloat16)
        return layer_out, proj_qkv[1], proj_qkv[2]

    weight_spec = P('fsdp')
    return jax.shard_map(local_layer, mesh=mesh, in_specs=(P(batch_axes),) + (weight_spec,) * 12, out_specs=(P(batch_axes), P(batch_axes), P(batch_axes)), check_vma=False)
```

profile of v0, /device:TPU:1, one launch (start us, length us, event | category | flops | bytes accessed | tf_op | source)
XLA Modules:
  0.0 521.0 jit_solution(1866602988516693966)
XLA Ops:
  10.0 0.9 dynamic-update-slice
  10.9 0.8 dynamic-update-slice.1
  15.1 0.9 dynamic-update-slice.6
  16.0 0.9 dynamic-update-slice.2
  16.8 71.4 %all-reduce.8 = (bf16[6912]{0:T(1024)(128)(2,1)S(1)}, bf16[2304]{0:T(1024)(128)(2,1)S(1)}, bf16[2304]{0:T(1024)(128)(2,1)S(1)}, bf16[2304]{0:T(1024)(128)(2,1)S(...) all-reduce(bf16[6912]{0:T(1024)(128)(2,1)S(1)} %dynamic-update-slic, ...), channel_id=1, replica_groups=mesh['dp'=1,'fsdp'=128] {'fsdp'}, use_global_device_ids=true, to_apply=%add.2 | all-reduce | flops 29952 | bytes 119808
  91.4 2.0 convert_reduce_fusion.1
  94.2 15.5 %reshape.176 = bf16[24,96,2304,1]{2,1,0,3:T(8,128)(2,1)} reshape(bf16[128,18,2304]{2,1,0:T(8,128)(2,1)} %all-gather.11.cloned.1.call-done) | data formatting | bytes 21233664 | tf_op jit(solution)/shard_map/reshape | solution.py:52
  109.8 103.7 %all-gather.7.cloned.1.call-done = bf16[2304,3,24,96]{3,2,1,0:T(8,128)(2,1)} async-done(((bf16[18,3,24,96]{3,2,1,0:T(8,128)(2,1)}), bf16[2304,3,24,96]{3,2,1,0:T(8,128)(2,1)}) %all-gather.7.cloned.1.call-update) | async-done | bytes 31850512 | tf_op jit(solution)/shard_map/all_gather | solution.py:41
  213.4 24.5 %fusion.42 = bf16[3,1,512,24,96]{2,4,3,0,1:T(8,128)(2,1)S(1)} fusion(f32[3,24,96]{2,1,0:T(8,128)S(1)} %reshape.150, bf16[2304,3,24,96]{3,2,1,0:T(8,128)(2,1)} %all-gather.7.cloned.1.call-done, bf16[1,512,2304]{2,1,0:T(8,128)(2,1)S(1)} %copy-done.1, f32[2304]{0:T(1024)S(1)} %convert_element_type.70, f32[2304]{0:T(1024)S(1)} %convert_element_type.69, ...), kind=kOutput, calls=%fused_computation.42 | convolution fusion | flops 16321609728 | bytes 41337856 | tf_op jit(solution)/shard_map/bsd,djhe->jbshe/dot_general | solution.py:49
  238.0 2.6 slice_bitcast_fusion
  240.6 41.5 %while.11 = (s32[]{:T(128)}, bf16[2,1,256,24,96]{2,4,3,1,0:T(8,128)(2,1)}, s32[2]{0:T(128)S(1)}, bf16[1,512,24,96]{1,3,2,0:T(8,128)(2,1)}, bf16[1,512,24,96]{1,3...) while((s32[]{:T(128)}, ...), condition=%wide.region_5.6_spmd.clone, body=%wide.region_2.5_spmd.clone.sunk | while | flops 1233847040 | bytes 57723560 | solution.py:34
  241.9 3.1 fusion.107
  245.2 8.8 %fusion.108 = (f32[24,256]{1,0:T(8,128)S(1)}, f32[24,256,512]{2,1,0:T(8,128)}) fusion(f32[24,256,512]{2,1,0:T(8,128)S(1)} %fusion.107, pred[256,512]{1,0:T(8,128)(4,1)S(1)} %iota_compare_fusion.2), kind=kOutput, calls=%fused_computation.89.clone.1 | output fusion | flops 18874880 | bytes 25321472 | tf_op jit(solution)/shard_map/while/body/eval_jaxpr/sub | solution.py:31
  254.1 7.3 %fusion.109 = bf16[2,1,256,24,96]{2,4,3,1,0:T(8,128)(2,1)} fusion(bf16[2,1,256,24,96]{2,4,3,1,0:T(8,128)(2,1)} %get-tuple-element.134, s32[]{:T(128)} %get-tuple-element.133, bf16[1,512,24,96]{1,3,2,0:T(8,128)(2,1)} %get-tuple-element.148, f32[24,256,512]{2,1,0:T(8,128)} %get-tuple-element.121, f32[24,256]{1,0:T(8,128)S(1)} %get-tuple-element.122), kind=kOutput, calls=%fused_computation.15.clone.1 | convolution fusion | flops 610861056 | bytes 16146944 | tf_op jit(solution)/shard_map/while/body/eval_jaxpr/bhqk,bkhe->bqhe/dot_general | solution.py:32
  262.7 3.1 fusion.107
  266.0 8.8 %fusion.108 = (f32[24,256]{1,0:T(8,128)S(1)}, f32[24,256,512]{2,1,0:T(8,128)}) fusion(f32[24,256,512]{2,1,0:T(8,128)S(1)} %fusion.107, pred[256,512]{1,0:T(8,128)(4,1)S(1)} %iota_compare_fusion.2), kind=kOutput, calls=%fused_computation.89.clone.1 | output fusion | flops 18874880 | bytes 25321472 | tf_op jit(solution)/shard_map/while/body/eval_jaxpr/sub | solution.py:31
  274.8 7.3 %fusion.109 = bf16[2,1,256,24,96]{2,4,3,1,0:T(8,128)(2,1)} fusion(bf16[2,1,256,24,96]{2,4,3,1,0:T(8,128)(2,1)} %get-tuple-element.134, s32[]{:T(128)} %get-tuple-element.133, bf16[1,512,24,96]{1,3,2,0:T(8,128)(2,1)} %get-tuple-element.148, f32[24,256,512]{2,1,0:T(8,128)} %get-tuple-element.121, f32[24,256]{1,0:T(8,128)S(1)} %get-tuple-element.122), kind=kOutput, calls=%fused_computation.15.clone.1 | convolution fusion | flops 610861056 | bytes 16146944 | tf_op jit(solution)/shard_map/while/body/eval_jaxpr/bhqk,bkhe->bqhe/dot_general | solution.py:32
  282.2 9.9 %fusion.67 = f32[2,256,2304,1]{2,1,3,0:T(8,128)S(1)} fusion(bf16[24,96,2304,1]{2,1,0,3:T(8,128)(2,1)} %reshape.176, bf16[2,1,256,24,96]{2,4,3,1,0:T(8,128)(2,1)} %get-tuple-element.40), kind=kOutput, calls=%fused_computation.71 | convolution fusion | flops 5435817984 | bytes 17694720 | tf_op jit(solution)/shard_map/nbqhe,hec->bnqc/dot_general | solution.py:54
  292.1 0.9 convert_reduce_fusion
  293.7 67.3 %all-gather.13.cloned.1.call-done = bf16[128,18,9216]{2,1,0:T(8,128)(2,1)} async-done(((bf16[1,18,9216]{2,1,0:T(8,128)(2,1)}), bf16[128,18,9216]{2,1,0:T(8,128)(2,1)}) %all-gather.13.cloned.1.call-update) | async-done | bytes 42467344 | tf_op jit(solution)/shard_map/all_gather | solution.py:41
  361.1 47.5 %reshape.170 = bf16[2304,9216]{1,0:T(8,128)(2,1)} reshape(bf16[128,18,9216]{2,1,0:T(8,128)(2,1)} %all-gather.13.cloned.1.call-done) | data formatting | bytes 84934656
  408.5 33.8 %fusion.34.clone.8 = bf16[512,9216]{1,0:T(8,128)(2,1)} fusion(bf16[2304,9216]{1,0:T(8,128)(2,1)} %reshape.170, f32[9216]{0:T(1024)S(1)} %copy-done.4, bf16[1,512,2304]{2,1,0:T(8,128)(2,1)S(1)} %get-tuple-element.76, f32[2304]{0:T(1024)S(1)} %copy-done.7, f32[2304]{0:T(1024)S(1)} %copy-done.6, ...), kind=kOutput, calls=%fused_computation.33.clone.clone.clone.clone.clone.clone.clone.1 | convolution fusion | flops 21797535744 | bytes 54323200 | tf_op jit(solution)/shard_map/bsd,df->bsf/dot_general | solution.py:59
  442.3 41.1 %all-gather.9.cloned.1.call-done = bf16[9216,2304]{1,0:T(8,128)(2,1)} async-done(((bf16[72,2304]{1,0:T(8,128)(2,1)}), bf16[9216,2304]{1,0:T(8,128)(2,1)}) %all-gather.9.cloned.1.call-update) | async-done | bytes 42467344 | tf_op jit(solution)/shard_map/all_gather | solution.py:41
  483.5 31.0 %fusion.61 = bf16[1,512,2304]{2,1,0:T(8,128)(2,1)} fusion(bf16[1,512,2304]{2,1,0:T(8,128)(2,1)S(1)} %get-tuple-element.76, bf16[9216,2304]{1,0:T(8,128)(2,1)} %all-gather.9.cloned.1.call-done, f32[2304]{0:T(1024)S(1)} %copy-done.5, bf16[512,9216]{1,0:T(8,128)(2,1)} %fusion.34.clone.8), kind=kOutput, calls=%fused_computation.65 | convolution fusion | flops 21747990528 | bytes 56632320 | tf_op jit(solution)/shard_map/bsf,fd->bsd/dot_general | solution.py:63
  (59 shorter events, 12.4 us)
Async XLA Ops:
  7.2 86.3 %copy-start.1 = (bf16[1,512,2304]{2,1,0:T(8,128)(2,1)S(1)}, bf16[1,512,2304]{2,1,0:T(8,128)(2,1)}, u32[]{:S(2)}) copy-start(bf16[1,512,2304]{2,1,0:T(8,128)(2,1)} %param.15) | copy-start | bytes 7077892
  7.2 87.0 %all-gather.11.cloned.1.call-start = ((), (), s32[]{:S(2)}) async-start(), calls=%async_computation.2 | async-start | bytes 14266368 | tf_op jit(solution)/shard_map/all_gather | solution.py:41
  7.9 205.5 %all-gather.7.cloned.1.call-start = ((), (), s32[]{:S(2)}) async-start(), calls=%async_computation | async-start | bytes 42799104 | tf_op jit(solution)/shard_map/all_gather | solution.py:41
  8.7 352.4 %all-gather.13.cloned.1.call-start = ((), (), s32[]{:S(2)}) async-start(), calls=%async_computation.3 | async-start | bytes 57065472 | tf_op jit(solution)/shard_map/all_gather | solution.py:41
  9.4 474.1 %all-gather.9.cloned.1.call-start = ((), (), s32[]{:S(2)}) async-start(), calls=%async_computation.1 | async-start | bytes 42799104 | tf_op jit(solution)/shard_map/all_gather | solution.py:41
  282.2 9.9 %copy-start = (bf16[1,512,24,96]{1,3,2,0:T(8,128)(2,1)}, bf16[1,512,24,96]{1,3,2,0:T(8,128)(2,1)S(1)}, u32[]{:S(2)}) copy-start(bf16[1,512,24,96]{1,3,2,0:T(8,128)(2,1)S(1)} %get-tuple-element.157) | copy-start | bytes 7077892
  282.2 9.9 %copy-start.2 = (bf16[1,512,2304]{2,1,0:T(8,128)(2,1)S(1)}, bf16[1,512,2304]{2,1,0:T(8,128)(2,1)}, u32[]{:S(2)}) copy-start(bf16[1,512,2304]{2,1,0:T(8,128)(2,1)} %param.15) | copy-start | bytes 7077892
  282.2 9.9 %copy-start.3 = (f32[2304]{0:T(1024)S(1)}, f32[2304]{0:T(1024)}, u32[]{:S(2)}) copy-start(f32[2304]{0:T(1024)} %convert_element_type.74) | copy-start | bytes 27652
  293.7 114.8 %copy-start.4 = (f32[9216]{0:T(1024)S(1)}, f32[9216]{0:T(1024)}, u32[]{:S(2)}) copy-start(f32[9216]{0:T(1024)} %convert_element_type.80) | copy-start | bytes 110596
  293.7 114.8 %copy-start.6 = (f32[2304]{0:T(1024)S(1)}, f32[2304]{0:T(1024)}, u32[]{:S(2)}) copy-start(f32[2304]{0:T(1024)} %convert_element_type.77) | copy-start | bytes 27652
  293.7 114.8 %copy-start.7 = (f32[2304]{0:T(1024)S(1)}, f32[2304]{0:T(1024)}, u32[]{:S(2)}) copy-start(f32[2304]{0:T(1024)} %convert_element_type.78) | copy-start | bytes 27652
  408.5 74.9 %copy-start.5 = (f32[2304]{0:T(1024)S(1)}, f32[2304]{0:T(1024)}, u32[]{:S(2)}) copy-start(f32[2304]{0:T(1024)} %convert_element_type.82) | copy-start | bytes 27652
Sparse Core Ops, SparseCore 0:
  11.0 79.7 all-gather.10
  93.8 119.5 all-gather.6
  216.5 144.5 all-gather.12
  363.9 119.4 all-gather.8
where the time goes:
time: 522 us; the launch traced here: 521 us
  waiting for transfers between devices  215 us (41%)
  matrix products  120 us (23%)
  local copies, waits for them, and re-layouts  73.9 us (14%)
  blocking collectives  71.4 us (14%)
  other arithmetic  25.4 us (5%)
  between operations  13.9 us (3%)
    all_gather x4, waiting for transfers between devices, gather_full(): return lax.all_gather(shard, 'fsdp', axis=0, tiled=True)  212 us
    unnamed x1, blocking collectives  71.4 us
    unnamed x33, local copies, waits for them, and re-layouts  54.3 us
    dot_general x1, matrix products, local_layer(): jnp.einsum('bsd,df->bsf', normed2, w_up_full, preferred_element_type=jnp....  33.8 us
    dot_general x1, matrix products, local_layer(): jnp.einsum('bsf,fd->bsd', hidden, w_down_full, preferred_element_type=jnp...  31 us
    dot_general x1, matrix products, local_layer(): jnp.einsum('bsd,djhe->jbshe', normed1, w_qkv_full, preferred_element_type...  24.5 us
    sub x2, other arithmetic, one_block(): probs = jax.nn.softmax(scores, axis=-1).astype(jnp.bfloat16)  17.6 us
    reshape x1, local copies, waits for them, and re-layouts, local_layer(): w_out_full = gather_full(w_out).reshape(heads, head_dim, d_model)  15.5 us
  transfers between devices with their start and end apart: 4, of which 3 were waited for; matrix products, arithmetic and copies ran while one was open for 36% of the time, Pallas kernels for 0%

commit v1 on v0

v1 whole, which is shorter than its diff:
```python
import functools

import jax
import jax.numpy as jnp
from jax import lax
from jax.experimental import pallas as pl
from jax.experimental.pallas import tpu as pltpu
from jax.sharding import PartitionSpec as P

LN_EPS = 1e-5
MESH = pl.DeviceIdType.MESH
BF = jnp.bfloat16
F32 = jnp.float32
CHUNKS = 9
SLOTS = 3


def layer_kernel(dims, x_ref, own, ln1g, ln1b, bqkv, bout, ln2g, ln2b, bup, bdown,
                 y_ref, kt_out, vt_out, G,
                 h, qkvt, ctxt, ctx, x1, a, wbuf, acc, R, S, LS, KS):
    seq, d, heads, hd, rows, lane = dims
    pair = 2 * lane
    me = lax.axis_index("fsdp")
    core = lax.rem(me, 2)
    cx = lax.rem(me // 2, 4)
    cy = lax.rem(me // 8, 4)
    cz = me // 32
    sib = me + 1 - 2 * core

    def pick(c, v0, v1, v2):
        return jnp.where(c == 0, v0, jnp.where(c == 1, v1, v2))

    def place(c):
        i0 = pick(c, cx, cy, cz)
        i1 = pick(c, cy, cz, cx)
        i2 = pick(c, cz, cx, cy)
        return i0, i1, i2

    def strides(c):
        return pick(c, 2, 8, 32), pick(c, 8, 32, 2), pick(c, 32, 2, 8)

    def near(i, stride):
        up = lax.rem(i + 1, 4)
        down = lax.rem(i + 3, 4)
        return me + (up - i) * stride, me + (down - i) * stride, up, down

    def send(src, dst, s, r, dev):
        pltpu.make_async_remote_copy(
            src_ref=src, dst_ref=dst, send_sem=s, recv_sem=r,
            device_id={"fsdp": dev}, device_id_type=MESH).start()

    def take(ref, sem):
        pltpu.make_async_copy(ref, ref, sem).wait()

    def colours(body):
        def step(c, carry):
            body(c)
            return carry
        lax.fori_loop(0, 3, step, 0)

    def slab(k, c):
        return (k * 2 + core) * 3 + c

    def p0_send(k):
        def body(c):
            i0, i1, i2 = place(c)
            right, left, _, _ = near(i0, strides(c)[0])
            dst = G.at[slab(k, c), i2, i1, i0]
            src = own.at[k * 3 + c]
            send(src, dst, S.at[k, 0], R.at[k * 3 + c, 0], right)
            send(src, dst, S.at[k, 0], R.at[k * 3 + c, 0], left)
        colours(body)

    def p0_forward(k):
        def body(c):
            i0, i1, i2 = place(c)
            right, left, up, down = near(i0, strides(c)[0])
            g = slab(k, c)
            take(G.at[g, 0, 0, pl.ds(0, 2)], R.at[k * 3 + c, 0])
            if k % 2 == 0:
                blk = G.at[g, i2, i1, down]
                send(blk, blk, S.at[k, 0], R.at[k * 3 + c, 1], right)
            else:
                blk = G.at[g, i2, i1, up]
                send(blk, blk, S.at[k, 0], R.at[k * 3 + c, 1], left)
        colours(body)

    def p0_done(k):
        colours(lambda c: take(G.at[slab(k, c), 0, 0, 0], R.at[k * 3 + c, 1]))

    def p1_send(k):
        def body(c):
            i0, i1, i2 = place(c)
            right, left, _, _ = near(i1, strides(c)[1])
            lo = G.at[slab(k, c), i2, i1, pl.ds(0, 2)]
            hi = G.at[slab(k, c), i2, i1, pl.ds(2, 2)]
            q = k * 3 + c
            send(lo, lo, S.at[k, 1], R.at[q, 2], right)
            send(hi, hi, S.at[k, 1], R.at[q, 2], left)
            send(hi, hi, S.at[k, 1], R.at[q, 3], right)
            send(lo, lo, S.at[k, 1], R.at[q, 3], left)
        colours(body)

    def p1_forward(k):
        def body(c):
            i0, i1, i2 = place(c)
            right, left, up, down = near(i1, strides(c)[1])
            g = slab(k, c)
            q = k * 3 + c
            take(G.at[g, 0, 0], R.at[q, 2])
            lo = G.at[g, i2, down, pl.ds(0, 2)]
            hi = G.at[g, i2, up, pl.ds(2, 2)]
            send(lo, lo, S.at[k, 1], R.at[q, 3], right)
            send(hi, hi, S.at[k, 1], R.at[q, 3], left)
        colours(body)

    def p1_done(k):
        colours(lambda c: take(G.at[slab(k, c), 0, pl.ds(0, 2)], R.at[k * 3 + c, 3]))

    def p2_first(k):
        def body(c):
            i0, i1, i2 = place(c)
            right, left, _, _ = near(i2, strides(c)[2])
            g = slab(k, c)
            lo = G.at[g, i2, pl.ds(0, 2)]
            hi = G.at[g, i2, pl.ds(2, 2)]
            send(lo, lo, S.at[k, 2], R.at[k * 3 + c, 4], right)
            send(hi, hi, S.at[k, 2], R.at[k * 3 + c, 4], left)
            send(G.at[g, i2], G.at[g, i2], S.at[k, 3], R.at[k * 3 + c, 6], sib)
        colours(body)

    def p2_second(k):
        def body(c):
            i0, i1, i2 = place(c)
            right, left, _, _ = near(i2, strides(c)[2])
            g = slab(k, c)
            lo = G.at[g, i2, pl.ds(0, 2)]
            hi = G.at[g, i2, pl.ds(2, 2)]
            send(hi, hi, S.at[k, 2], R.at[k * 3 + c, 5], right)
            send(lo, lo, S.at[k, 2], R.at[k * 3 + c, 5], left)
        colours(body)

    def p2_forward(k):
        def body(c):
            i0, i1, i2 = place(c)
            right, left, up, down = near(i2, strides(c)[2])
            g = slab(k, c)
            q = k * 3 + c
            take(G.at[g, 0], R.at[q, 4])
            lo = G.at[g, down, pl.ds(0, 2)]
            hi = G.at[g, up, pl.ds(2, 2)]
            send(lo, lo, S.at[k, 2], R.at[q, 5], right)
            send(hi, hi, S.at[k, 2], R.at[q, 5], left)
        colours(body)

    def p2_done(k):
        def body(c):
            i0, i1, i2 = place(c)
            g = slab(k, c)
            take(G.at[g, pl.ds(0, 2)], R.at[k * 3 + c, 5])
            for o in range(1, 4):
                part = G.at[g, lax.rem(i2 + o, 4)]
                send(part, part, S.at[k, 3], R.at[k * 3 + c, 6], sib)
        colours(body)

    def sibling_done(k):
        colours(lambda c: take(G.at[slab(k, c)], R.at[k * 3 + c, 6]))

    def issue(t):
        if t + 2 < CHUNKS:
            p0_send(t + 2)
        if t + 1 < CHUNKS:
            p1_send(t + 1)
        if t < CHUNKS:
            p2_first(t)

    def visit1(t):
        if t >= 1:
            p2_done(t - 1)
        if t + 2 < CHUNKS:
            p0_forward(t + 2)
        if t + 1 < CHUNKS:
            p1_forward(t + 1)
        p2_second(t)

    def visit2(t):
        p2_forward(t)
        if t + 2 < CHUNKS:
            p0_done(t + 2)
        if t + 1 < CHUNKS:
            p1_done(t + 1)
        issue(t + 1)
        if t >= 1:
            sibling_done(t - 1)

    def load_cols(k, u, slot):
        x = u // 3
        c = lax.rem(u, 3)
        for s in range(2):
            g = (k * 2 + s) * 3 + c
            dst = wbuf.at[slot, :, :, :, pl.ds(s * lane, lane)]

            @pl.when(c == 0)
            def _():
                pltpu.make_async_copy(G.at[g, :, :, x], dst, LS.at[slot]).start()

            @pl.when(c == 1)
            def _():
                pltpu.make_async_copy(G.at[g, x], dst, LS.at[slot]).start()

            @pl.when(c == 2)
            def _():
                for y in range(4):
                    pltpu.make_async_copy(
                        G.at[g, y, x], wbuf.at[slot, :, y, :, pl.ds(s * lane, lane)], LS.at[slot]).start()

    def load_rows(k, u, slot):
        c = u // 4
        z = lax.rem(u, 4)
        for s in range(2):
            g = (k * 2 + s) * 3 + c
            dst = wbuf.at[slot, :, :, :, pl.ds(s * lane, lane)]

            @pl.when(c == 0)
            def _():
                pltpu.make_async_copy(G.at[g, z], dst, LS.at[slot]).start()

            @pl.when(c == 1)
            def _():
                for x in range(4):
                    pltpu.make_async_copy(
                        G.at[g, x, z], wbuf.at[slot, :, x, :, pl.ds(s * lane, lane)], LS.at[slot]).start()

            @pl.when(c == 2)
            def _():
                pltpu.make_async_copy(G.at[g, :, :, z], dst, LS.at[slot]).start()

    def run_units(load, k, lo, hi, body):
        load(k, lo, lo % SLOTS)
        load(k, lo + 1, (lo + 1) % SLOTS)

        def step(u, carry):
            slot = lax.rem(u, SLOTS)
            take(wbuf.at[slot], LS.at[slot])

            @pl.when(u + 2 < hi)
            def _():
                load(k, u + 2, lax.rem(u + 2, SLOTS))
            body(u, slot)
            return carry
        lax.fori_loop(lo, hi, step, 0)

    def weight(slot):
        return wbuf[slot].reshape(d, pair)

    def qkv_unit(k):
        def body(u, slot):
            p = 12 * k + u
            r = jnp.dot(h[...], weight(slot), preferred_element_type=F32) + bqkv[p]
            qkvt[pl.ds(pl.multiple_of(p * pair, pair), pair), :] = r.astype(BF).T
        return body

    def out_unit(u, slot):
        p = u - 3
        cols = pl.ds(pl.multiple_of(p * pair, pair), pair)
        r = jnp.dot(ctx[...], weight(slot), preferred_element_type=F32)
        x1[:, cols] = (x_ref[:, cols].astype(F32) + r + bout[p]).astype(BF)

    def up_unit(k):
        def body(u, slot):
            p = 12 * (k - 3) + u
            cols = pl.ds(pl.multiple_of(p * pair, pair), pair)
            r = jnp.dot(h[...], weight(slot), preferred_element_type=F32) + bup[p]
            a[:, cols] = jax.nn.gelu(r, approximate=True).astype(BF)
        return body

    def down_unit(k):
        def body(u, slot):
            c = u // 4
            z = lax.rem(u, 4)
            p = 3 * (k - 6) + c
            cols = pl.ds(pl.multiple_of(p * pair, pair), pair)
            r = jnp.dot(a[:, pl.ds(pl.multiple_of(z * d, lane), d)], weight(slot), preferred_element_type=F32)

            @pl.when(z == 0)
            def _():
                acc[...] = r

            @pl.when(z > 0)
            def _():
                acc[...] += r

            @pl.when(z == 3)
            def _():
                y_ref[:, cols] = (x1[:, cols].astype(F32) + acc[...] + bdown[p]).astype(BF)
        return body

    def norm(src, gain, shift):
        n = seq // 8

        def step(b, carry):
            at = pl.ds(pl.multiple_of(b * n, n), n)
            v = src[at, :].astype(F32)
            v = v - jnp.mean(v, axis=-1, keepdims=True)
            var = jnp.mean(v * v, axis=-1, keepdims=True)
            h[at, :] = (v * lax.rsqrt(var + LN_EPS) * gain[...] + shift[...]).astype(BF)
            return carry
        lax.fori_loop(0, 8, step, 0)

    def attend(lo, hi):
        qb = seq // 2
        scale = hd ** -0.5

        def step(i, carry):
            q_rows = pl.ds(pl.multiple_of(i * hd, hd), hd)
            k_rows = pl.ds(pl.multiple_of(i * hd + d, hd), hd)
            v_rows = pl.ds(pl.multiple_of(i * hd + 2 * d, hd), hd)
            for b in range(2):
                n = (b + 1) * qb
                q = qkvt[q_rows, b * qb:n]
                s = lax.dot_general(q, qkvt[k_rows, :n], (((0,), (0,)), ((), ())),
                                    preferred_element_type=F32) * scale
                row = lax.broadcasted_iota(jnp.int32, (qb, n), 0) + b * qb
                col = lax.broadcasted_iota(jnp.int32, (qb, n), 1)
                s = jnp.where(col <= row, s, -jnp.inf)
                e = jnp.exp(s - jnp.max(s, axis=-1, keepdims=True))
                w = (e / jnp.sum(e, axis=-1, keepdims=True)).astype(BF)
                o = lax.dot_general(qkvt[v_rows, :n], w, (((1,), (1,)), ((), ())),
                                    preferred_element_type=F32)
                ctxt[q_rows, b * qb:n] = o.astype(BF)
            return carry
        lax.fori_loop(lo, hi, step, 0)

    def flip():
        def step(i, carry):
            at = pl.ds(pl.multiple_of(i * pair, pair), pair)
            ctx[:, at] = ctxt[at, :].T
            return carry
        lax.fori_loop(0, d // pair, step, 0)

    def cache_copy(which):
        out = kt_out if which == 0 else vt_out
        return pltpu.make_async_copy(qkvt.at[pl.ds((which + 1) * d, d)], out, KS.at[which])

    p0_send(0)
    p0_send(1)

    def put(q, carry):
        c = lax.rem(q, 3)
        i0, i1, i2 = place(c)
        pltpu.make_async_copy(own.at[q], G.at[slab(q // 3, c), i2, i1, i0], KS.at[2]).start()
        return carry
    lax.fori_loop(0, 27, put, 0)
    take(G.at[pl.ds(0, 27), 0, 0, 0], KS.at[2])
    p0_forward(0)
    p0_forward(1)
    p0_done(0)
    p1_send(0)
    p1_forward(0)
    p0_done(1)
    p1_done(0)
    issue(0)
    norm(x_ref, ln1g, ln1b)
    visit1(0)
    visit2(0)

    visit1(1)
    visit2(1)
    run_units(load_cols, 0, 0, 12, qkv_unit(0))
    visit1(2)
    visit2(2)
    run_units(load_cols, 1, 0, 12, qkv_unit(1))
    visit1(3)
    visit2(3)
    run_units(load_cols, 2, 0, 3, qkv_unit(2))
    a1 = heads * 5 // 12
    a2 = heads * 9 // 12
    attend(0, a1)
    visit1(4)
    attend(a1, a2)
    visit2(4)
    attend(a2, heads)
    cache_copy(0).start()
    cache_copy(1).start()
    flip()
    run_units(load_cols, 2, 3, 12, out_unit)
    visit1(5)
    norm(x1, ln2g, ln2b)
    run_units(load_cols, 3, 0, 12, up_unit(3))
    visit2(5)
    run_units(load_cols, 4, 0, 12, up_unit(4))
    visit1(6)
    visit2(6)
    run_units(load_cols, 5, 0, 12, up_unit(5))
    visit1(7)
    visit2(7)
    run_units(load_rows, 6, 0, 12, down_unit(6))
    visit1(8)
    visit2(8)
    run_units(load_rows, 7, 0, 12, down_unit(7))
    p2_done(8)
    sibling_done(8)
    run_units(load_rows, 8, 0, 12, down_unit(8))

    cache_copy(0).wait()
    cache_copy(1).wait()
    for k in range(CHUNKS):
        take(G.at[pl.ds(0, 3), 0, 0, pl.ds(0, 3)], S.at[k, 0])
        take(G.at[pl.ds(0, 3), 0, pl.ds(0, 3)], S.at[k, 1])
        take(G.at[pl.ds(0, 3), pl.ds(0, 3)], S.at[k, 2])
        take(G.at[pl.ds(0, 3)], S.at[k, 3])


def solution(mesh):
    batch_axes = ('dp', 'fsdp')
    n_dev = mesh.shape['fsdp']

    def exchange(blocks, size):
        groups = [list(range(i, i + size)) for i in range(0, n_dev, size)]
        return lax.all_to_all(blocks, 'fsdp', 0, 0, axis_index_groups=groups, tiled=True)

    def local_layer(prompts, ln1_gain, ln1_bias, w_qkv, b_qkv, w_out, b_out, ln2_gain, ln2_bias, w_up, b_up, w_down, b_down):
        _, seq, d = prompts.shape
        heads, hd = w_qkv.shape[2], w_qkv.shape[3]
        lane = d // 18
        rows = d // 16
        pair = 2 * lane
        r = w_up.shape[0]

        parts = [ln1_gain, ln1_bias, b_out, ln2_gain, ln2_bias, b_down, b_qkv, b_up]
        packed = jnp.concatenate(parts)
        total = packed.shape[0]
        packed = jnp.pad(packed, (0, -total % 128))
        packed = lax.all_gather(packed, 'fsdp', axis=0)
        vecs, at = [], 0
        for part in parts:
            vecs.append(packed[:, at:at + part.shape[0]].reshape(-1).astype(F32))
            at += part.shape[0]
        g1, s1, bo, g2, s2, bd, bq, bu = vecs

        w1 = jnp.concatenate([w_qkv.reshape(r, -1), w_out], axis=1)
        w12 = jnp.stack([w1, w_up]).reshape(2, r, 3, 4, 3, 2, lane)
        w12 = w12.transpose(3, 5, 0, 2, 4, 1, 6).reshape(8, 18 * r, lane)
        w12 = exchange(w12, 8).reshape(8, 18, r, lane).transpose(1, 0, 2, 3).reshape(18, rows, lane)
        w3 = w_down.reshape(-1, 9, 2, lane).transpose(2, 1, 0, 3).reshape(2, -1, lane)
        w3 = exchange(w3, 2).reshape(2, 9, -1, lane).transpose(1, 0, 2, 3).reshape(9, rows, lane)
        own = jnp.concatenate([w12, w3], axis=0)

        dims = (seq, d, heads, hd, rows, lane)
        vm = pl.BlockSpec(memory_space=pltpu.VMEM)
        hbm = pl.BlockSpec(memory_space=pl.ANY)
        y, kt, vt, _ = pl.pallas_call(
            functools.partial(layer_kernel, dims),
            out_shape=(
                jax.ShapeDtypeStruct((seq, d), BF),
                jax.ShapeDtypeStruct((d, seq), BF),
                jax.ShapeDtypeStruct((d, seq), BF),
                jax.ShapeDtypeStruct((6 * CHUNKS, 4, 4, 4, rows, lane), BF),
            ),
            in_specs=[vm] * 10,
            out_specs=(vm, hbm, hbm, hbm),
            scratch_shapes=[
                pltpu.VMEM((seq, d), BF),
                pltpu.VMEM((3 * d, seq), BF),
                pltpu.VMEM((d, seq), BF),
                pltpu.VMEM((seq, d), BF),
                pltpu.VMEM((seq, d), BF),
                pltpu.VMEM((seq, 4 * d), BF),
                pltpu.VMEM((SLOTS, 4, 4, rows, pair), BF),
                pltpu.VMEM((seq, pair), F32),
                pltpu.SemaphoreType.DMA((3 * CHUNKS, 7)),
                pltpu.SemaphoreType.DMA((CHUNKS, 4)),
                pltpu.SemaphoreType.DMA((SLOTS,)),
                pltpu.SemaphoreType.DMA((3,)),
            ],
            compiler_params=pltpu.CompilerParams(
                has_side_effects=True, vmem_limit_bytes=62 * 1024 * 1024),
            name="layer",
        )(prompts[0], own, g1[None], s1[None], bq.reshape(-1, 1, pair), bo.reshape(-1, 1, pair),
          g2[None], s2[None], bu.reshape(-1, 1, pair), bd.reshape(-1, 1, pair))
        kc = kt.reshape(heads, hd, seq).transpose(2, 0, 1)[None]
        vc = vt.reshape(heads, hd, seq).transpose(2, 0, 1)[None]
        return y[None], kc, vc

    weight_spec = P('fsdp')
    return jax.shard_map(local_layer, mesh=mesh, in_specs=(P(batch_axes),) + (weight_spec,) * 12, out_specs=(P(batch_axes), P(batch_axes), P(batch_axes)), check_vma=False)
```

time: 522 us -> 353 us (0.68)
  Pallas kernels: 0 us -> 274 us
  waiting for transfers between devices: 215 us -> 4.46 us
  matrix products: 120 us -> 0 us
  local copies, waits for them, and re-layouts: 73.9 us -> 23.2 us
  blocking collectives: 71.4 us -> 37.5 us
  other arithmetic: 25.4 us -> 2.27 us
  between operations: 13.9 us -> 0.8 us
  starting transfers between devices: 0.15 us -> 8.88 us
    pallas_call x0 -> x1, Pallas kernels: none -> 274 us  [local_layer(): pl.pallas_call(functools.partial(layer_kernel, dims), out_shape=(jax.Shap...]
    all_gather x4 -> x0, waiting for transfers between devices: 212 us -> none  [gather_full(): return lax.all_gather(shard, 'fsdp', axis=0, tiled=True)]
    dot_general x8 -> x0, matrix products: 120 us -> none  [the longest x1 33.8 us: local_layer(): jnp.einsum('bsd,df->bsf', normed2, w_up_full, preferred_element_type=jnp....]
    unnamed x1 -> x0, blocking collectives: 71.4 us -> none
    unnamed x33 -> x15, local copies, waits for them, and re-layouts: 54.3 us -> 7.33 us
    all_gather x0 -> x1, blocking collectives: none -> 37.5 us  [local_layer(): packed = lax.all_gather(packed, 'fsdp', axis=0)]
    sub x2 -> x0, other arithmetic: 17.6 us -> none  [one_block(): probs = jax.nn.softmax(scores, axis=-1).astype(jnp.bfloat16)]
    reshape x1 -> x4, local copies, waits for them, and re-layouts: 15.5 us -> 2.62 us  [the longest x1 1.13 us: local_layer(): w_down.reshape(-1, 9, 2, lane).transpose(2, 1, 0, 3).reshape(2, -1, lane)]
  transfers between devices with their start and end apart: 4 -> 2, of which waited for: 3 -> 1; matrix products, arithmetic and copies ran while one was open for 36% -> 4% of each run, Pallas kernels for 0% -> 0%
where the time goes in v1:
time: 353 us; the launch traced here: 352 us
  Pallas kernels  274 us (78%)
  blocking collectives  37.5 us (11%)
  local copies, waits for them, and re-layouts  23.2 us (7%)
  starting transfers between devices  8.88 us (3%)
  waiting for transfers between devices  4.46 us (1%)
    pallas_call x1, Pallas kernels, local_layer(): pl.pallas_call(functools.partial(layer_kernel, dims), out_shape=(jax.Shap...  274 us
    all_gather x1, blocking collectives, local_layer(): packed = lax.all_gather(packed, 'fsdp', axis=0)  37.5 us
    all_to_all x2, starting transfers between devices, exchange(): lax.all_to_all(blocks, 'fsdp', 0, 0, axis_index_groups=groups, tiled=True)  8.88 us
    unnamed x15, local copies, waits for them, and re-layouts  7.33 us
  transfers between devices with their start and end apart: 2, of which 1 were waited for; matrix products, arithmetic and copies ran while one was open for 4% of the time, Pallas kernels for 0%

profile of v1, /device:TPU:1, one launch (start us, length us, event | category | flops | bytes accessed | tf_op | source)
XLA Modules:
  0.0 351.6 jit_solution(11970530339078261235)
XLA Ops:
  0.7 1.1 reshape.153
  1.8 0.8 copy.45
  2.6 4.8 %all-to-all-start.1 = ((bf16[2,648,128]{2,1,0:T(8,128)(2,1)}), bf16[2,648,128]{2,1,0:T(8,128)(2,1)S(1)}, u32[]{:S(2)}, u32[]{:S(2)}) async-start(bf16[2,648,128]{2,1,0:T(8,128)(2,1)} %bitcast.6), calls=%async_computation.1 | async-start | bytes 663552 | tf_op jit(solution)/shard_map/all_to_all | solution.py:420
  7.4 5.4 %concatenate.12 = bf16[234]{0:T(256)(128)(2,1)S(1)} concatenate(bf16[18]{0:T(256)(128)(2,1)} %param.14, bf16[18]{0:T(256)(128)(2,1)} %param.15, bf16[18]{0:T(256)(128)(2,1)} %param.19, bf16[18]{0:T(256)(128)(2,1)} %param.20, bf16[18]{0:T(256)(128)(2,1)} %param.21, bf16[18]{0:T(256)(128)(2,1)} %param.25, bf16[54]{0:T(256)(128)(2,1)} %param.17, bf16[72]{0:T(256)(128)(2,1)} %param.23), dimensions={0} | concatenate | bytes 936 | tf_op jit(solution)/shard_map/concatenate | solution.py:431
  12.8 37.5 %all-gather.1 = bf16[128,1,256]{2,1,0:T(2,128)(2,1)S(1)} all-gather(bf16[1,1,256]{2,1,0:T(2,128)(2,1)S(1)} %reshape.168), channel_id=2, replica_groups=mesh['dp'=1,'fsdp'=128] {'fsdp'}, dimensions={0}, use_global_device_ids=true | all-gather | bytes 66048 | tf_op jit(solution)/shard_map/all_gather | solution.py:434
  51.1 0.9 maximum_bitcast_fusion
  52.1 0.5 copy.41
  52.5 0.9 copy.42
  53.5 4.1 %all-to-all-start = ((bf16[8,324,128]{2,1,0:T(8,128)(2,1)}), bf16[8,324,128]{2,1,0:T(8,128)(2,1)S(1)}, u32[]{:S(2)}, u32[]{:S(2)}) async-start(bf16[8,324,128]{2,1,0:T(8,128)(2,1)} %copy.42), calls=%async_computation | async-start | bytes 1343488 | tf_op jit(solution)/shard_map/all_to_all | solution.py:420
  57.6 0.8 reshape.171.bqkv
  58.5 0.7 reshape.173.bup
  59.4 0.7 reshape.174.bdown
  60.1 0.7 reshape.164.ln2b
  60.8 0.7 reshape.163.ln2g
  61.6 0.7 reshape.172.bout
  62.3 0.7 reshape.160.ln1b
  63.1 0.7 reshape.159.ln1g
  63.8 4.5 %all-to-all-done = bf16[8,324,128]{2,1,0:T(8,128)(2,1)S(1)} async-done(((bf16[8,324,128]{2,1,0:T(8,128)(2,1)}), bf16[8,324,128]{2,1,0:T(8,128)(2,1)S(1)}, u32[]{:S(2)}, u32[]{:S(2)}) %all-to-all-start) | async-done | bytes 663584 | tf_op jit(solution)/shard_map/all_to_all | solution.py:420
  68.8 1.0 pad_maximum_fusion.own
  69.8 274.4 %layer.1 = (bf16[512,2304]{1,0:T(8,128)(2,1)}, bf16[2304,512]{1,0:T(8,128)(2,1)}, bf16[2304,512]{1,0:T(8,128)(2,1)}, bf16[54,4,4,4,144,128]{5,4,3,2,1,0:T(8,128)(2,1)}) custom-call(bf16[512,2304]{1,0:T(8,128)(2,1)} %bitcast.31, bf16[27,144,128]{2,1,0:T(8,128)(2,1)} %pad_maximum_fusion.own, f32[1,2304]{1,0:T(1,128)} %reshape.159.ln1g, ...), custom_call_target="tpu_custom_call" | custom-call | tf_op jit(solution)/shard_map/layer/pallas_call | solution.py:452
  344.3 3.4 copy.57
  347.6 1.4 copy.58
  349.0 1.1 copy-done
  350.2 1.4 copy.59
  (24 shorter events, 1.5 us)
Async XLA Ops:
  0.6 49.7 %copy-start.3 = (bf16[18,3,24,96]{3,2,1,0:T(8,128)(2,1)S(1)}, bf16[18,3,24,96]{3,2,1,0:T(8,128)(2,1)}, u32[]{:S(2)}) copy-start(bf16[18,3,24,96]{3,2,1,0:T(8,128)(2,1)} %param.16) | copy-start | bytes 746500
  0.6 50.1 %copy-start.4 = (bf16[18,2304]{1,0:T(8,128)(2,1)S(1)}, bf16[18,2304]{1,0:T(8,128)(2,1)}, u32[]{:S(2)}) copy-start(bf16[18,2304]{1,0:T(8,128)(2,1)} %param.18) | copy-start | bytes 248836
  0.7 50.3 %copy-start.2 = (bf16[18,9216]{1,0:T(8,128)(2,1)S(1)}, bf16[18,9216]{1,0:T(8,128)(2,1)}, u32[]{:S(2)}) copy-start(bf16[18,9216]{1,0:T(8,128)(2,1)} %param.22) | copy-start | bytes 995332
  2.6 50.9 %all-to-all-start.1 = ((bf16[2,648,128]{2,1,0:T(8,128)(2,1)}), bf16[2,648,128]{2,1,0:T(8,128)(2,1)S(1)}, u32[]{:S(2)}, u32[]{:S(2)}) async-start(bf16[2,648,128]{2,1,0:T(8,128)(2,1)} %bitcast.6), calls=%async_computation.1 | async-start | bytes 663552 | tf_op jit(solution)/shard_map/all_to_all | solution.py:420
  53.5 14.8 %all-to-all-start = ((bf16[8,324,128]{2,1,0:T(8,128)(2,1)}), bf16[8,324,128]{2,1,0:T(8,128)(2,1)S(1)}, u32[]{:S(2)}, u32[]{:S(2)}) async-start(bf16[8,324,128]{2,1,0:T(8,128)(2,1)} %copy.42), calls=%async_computation | async-start | bytes 1343488 | tf_op jit(solution)/shard_map/all_to_all | solution.py:420
  344.3 3.4 copy-start.1
  347.6 2.5 copy-start

commit v2 on v0

v2 whole, which is shorter than its diff:
```python
import functools

import jax
import jax.numpy as jnp
import numpy as np
from jax import lax
from jax.experimental import pallas as pl
from jax.experimental.pallas import tpu as pltpu
from jax.sharding import PartitionSpec as P

LN_EPS = 1e-5
MESH = pl.DeviceIdType.MESH
BF = jnp.bfloat16
F32 = jnp.float32
CHUNKS = 9
SLOTS = 3
LO, HI, ALL3 = pl.ds(0, 2), pl.ds(2, 2), pl.ds(0, 3)
FIRST, SECOND, ACROSS, SIBLING = range(4)
ZEROS = (0, 0, 0)
THREE = range(3)
UNITS = 12
LANES = 128
LATE = (3, 4, 5)


def loop(hi, body, lo=0):
    def step(i, carry):
        body(i)
        return carry
    lax.fori_loop(lo, hi, step, None)


def wrap(i):
    return lax.rem(i, 4)


def layer_kernel(dims, x_ref, w1, w2, w3, vec, tab,
                 y_ref, kv_ref, G12, G3,
                 h, qt, ctxt, ctx, x1, a, wbuf, wbuf3, acc, own12, own3, stage12, stage3, V, lnv, bqkv, bout, bup, bdown, vrow,
                 R, S, LS, OS, X, XS, VR, VS):
    seq, d, heads, hd, rows, lane = dims
    pair = 2 * lane
    me = lax.axis_index("fsdp")
    core = lax.rem(me, 2)
    cx = wrap(me // 2)
    cy = wrap(me // 8)
    cz = me // 32
    sib = me + 1 - 2 * core
    spot = lax.rem(me, 8)

    class Block:
        def __init__(self, k):
            self.ref = G12 if k < 6 else G3
            self.base = k if k < 6 else k - 6

        def slab(self, c):
            return (self.base * 2 + core) * 3 + c

        def own(self, c):
            return (own12 if self.ref is G12 else own3).at[self.base * 3 + c]

    def pick(c, v):
        return jnp.where(c == 0, v[0], jnp.where(c == 1, v[1], v[2]))

    def place(c):
        v = (cx, cy, cz)
        return tuple(pick(c, v[p:] + v[:p]) for p in THREE)

    def near(c, p):
        v = (2, 8, 32)
        stride = pick(c, v[p:] + v[:p])
        i = place(c)[p]
        up, down = wrap(i + 1), wrap(i + 3)
        return me + (up - i) * stride, me + (down - i) * stride, up, down

    def send(src, dst, s, r, dev):
        pltpu.make_async_remote_copy(
            src_ref=src, dst_ref=dst, send_sem=s, recv_sem=r,
            device_id={"fsdp": dev}, device_id_type=MESH).start()

    def take(ref, sem):
        pltpu.make_async_copy(ref, ref, sem).wait()

    def colours(body):
        loop(3, body)

    def await_group(k, p, role, n=None):
        B = Block(k)

        def body(c):
            at = (B.slab(c),) + ZEROS[:3 - p]
            if n is not None:
                at = at[:-1] + (n,)
            take(B.ref.at[at], R.at[k * 3 + c, p, role])
        colours(body)

    def await_siblings(k, *roles):
        for role in roles:
            B = Block(k)
            part = LO if role == SECOND else 0
            colours(lambda c: take(B.ref.at[B.slab(c), part], R.at[k * 3 + c, SIBLING, role]))

    def p0_send(k):
        B = Block(k)

        def body(c):
            i0, i1, i2 = place(c)
            right, left, _, _ = near(c, 0)
            dst = B.ref.at[B.slab(c), i2, i1, i0]
            for dev in (right, left):
                send(B.own(c), dst, S.at[k, 0], R.at[k * 3 + c, 0, FIRST], dev)
            pltpu.make_async_copy(B.own(c), dst, OS.at[k]).start()
        colours(body)

    def p0_forward(k):
        B = Block(k)
        take(B.ref.at[0, 0, 0, ALL3], OS.at[k])
        await_group(k, 0, FIRST, LO)

        def body(c):
            i0, i1, i2 = place(c)
            right, left, up, down = near(c, 0)
            from_, to = (down, right) if k % 2 == 0 else (up, left)
            blk = B.ref.at[B.slab(c), i2, i1, from_]
            send(blk, blk, S.at[k, 0], R.at[k * 3 + c, 0, ACROSS], to)
        colours(body)

    def halves(k, c, p, i):
        B = Block(k)
        at = (B.slab(c), place(c)[2], i) if p == 1 else (B.slab(c), i)
        return B.ref.at[at + (LO,)], B.ref.at[at + (HI,)]

    def to_sibling(k, c, ahead, role):
        B = Block(k)
        part = B.ref.at[B.slab(c), wrap(place(c)[2] + ahead)]
        send(part, part, S.at[k, SIBLING], R.at[k * 3 + c, SIBLING, role], sib)

    def axis_first(k, p):
        def body(c):
            right, left, _, _ = near(c, p)
            lo, hi = halves(k, c, p, place(c)[p])
            send(lo, lo, S.at[k, p], R.at[k * 3 + c, p, FIRST], right)
            send(hi, hi, S.at[k, p], R.at[k * 3 + c, p, FIRST], left)
            if p == 2:
                to_sibling(k, c, 0, FIRST)
        colours(body)

    def axis_second(k, p):
        def body(c):
            right, left, _, _ = near(c, p)
            lo, hi = halves(k, c, p, place(c)[p])
            send(hi, hi, S.at[k, p], R.at[k * 3 + c, p, SECOND], right)
            send(lo, lo, S.at[k, p], R.at[k * 3 + c, p, SECOND], left)
        colours(body)

    def axis_forward(k, p):
        await_group(k, p, FIRST)

        def body(c):
            right, left, up, down = near(c, p)
            lo, hi = halves(k, c, p, down)[0], halves(k, c, p, up)[1]
            send(lo, lo, S.at[k, p], R.at[k * 3 + c, p, ACROSS], right)
            send(hi, hi, S.at[k, p], R.at[k * 3 + c, p, ACROSS], left)
        colours(body)

    def sides_in(k):
        await_group(k, 2, SECOND)

        def body(c):
            to_sibling(k, c, 1, SECOND)
            to_sibling(k, c, 3, SECOND)
        colours(body)

    def across_in(k):
        await_group(k, 2, ACROSS)
        colours(lambda c: to_sibling(k, c, 2, ACROSS))

    def x_send(k):
        src = w1 if k < 3 else w2
        j = k % 3

        def part(i, c):
            tile = 24 * j + 6 * (i // 2) + 2 * c + lax.rem(i, 2)
            return src.at[:, pl.ds(pl.multiple_of(tile * lane, lane), lane)]

        def body(o):
            i = lax.rem(spot + o, 8)
            for c in THREE:
                send(part(i, c), stage12.at[spot, 3 * k + c], XS.at[k], X.at[k], me - spot + i)
        loop(8, body, 1)
        for c in THREE:
            pltpu.make_async_copy(part(spot, c), stage12.at[spot, 3 * k + c], X.at[k]).start()

    def x_blocks(k):
        take(stage12.at[:, pl.ds(3 * k, 3)], X.at[k])
        for c in THREE:
            q = 3 * k + c
            own12[q] = jnp.concatenate([stage12[i, q].astype(F32) for i in range(8)], axis=0).astype(BF)

    def x3_send():
        for j in THREE:
            part = lambda s: w3.at[:, pl.ds(pl.multiple_of((2 * j + s) * 3 * lane, lane), 3 * lane)]
            send(part(1 - core), stage3.at[core, j], XS.at[6], X.at[6], sib)
            pltpu.make_async_copy(part(core), stage3.at[core, j], X.at[6]).start()

    def x3_blocks():
        take(stage3, X.at[6])
        n = rows // 3
        for j in THREE:
            both = jnp.concatenate([stage3[0, j].astype(F32), stage3[1, j].astype(F32)], axis=0)
            for c in THREE:
                own3[3 * j + c] = both[c * n:(c + 1) * n].astype(BF)

    def v_send(axis):
        if axis == 0:
            for o in range(1, 8):
                send(vec, V.at[cz, cy, spot], VS.at[0], VR.at[0], me - spot + lax.rem(spot + o, 8))
            pltpu.make_async_copy(vec, V.at[cz, cy, spot], VR.at[0]).start()
        elif axis == 1:
            take(V.at[0, 0], VR.at[0])
            for o in range(1, 4):
                send(V.at[cz, cy], V.at[cz, cy], VS.at[1], VR.at[1], me + (wrap(cy + o) - cy) * 8)
        else:
            take(V.at[0, pl.ds(0, 3)], VR.at[1])
            for o in range(1, 4):
                send(V.at[cz], V.at[cz], VS.at[2], VR.at[2], me + (wrap(cz + o) - cz) * 32)

    def spread(vals, at):
        n = at.size
        select = (lax.broadcasted_iota(jnp.int32, (LANES, n), 0) == tab[1:2, at]).astype(BF)
        return jnp.dot(vals, select, preferred_element_type=F32)

    def v_rows():
        take(V.at[ALL3], VR.at[2])
        nd = d // pair

        def body(t):
            at = pl.ds(pl.multiple_of(t * pair, pair), pair)
            m = spread(V[...].reshape(-1, LANES), at).reshape(LANES, 8, pair)
            dev = lax.broadcasted_iota(jnp.int32, m.shape, 0)
            v = jnp.sum(jnp.where(dev == tab[0:1, at][None], m, 0.0), axis=0)
            for i, src in enumerate((0, 1, 3, 4)):
                lnv[i, :, at] = v[src:src + 1]
            bout[t] = v[2:3]
            bdown[:, at] = v[5:6]
        loop(nd, body)
        dev = lax.broadcasted_iota(jnp.int32, (LANES, 8 * LANES), 0)
        slot = lax.broadcasted_iota(jnp.int32, (LANES, 8 * LANES), 1)
        for i in range(2):
            take_row = (slot == dev * 8 + 6 + i).astype(BF)
            vrow[i] = jnp.dot(take_row, V[...].reshape(-1, LANES), preferred_element_type=F32).astype(BF)

    def v_long(i, out, first, count):
        wide = 3 * pair

        def body(t):
            at = pl.ds(pl.multiple_of(first + t * wide, pair), wide)
            m = spread(vrow[i], at)
            dev = lax.broadcasted_iota(jnp.int32, m.shape, 0)
            v = jnp.sum(jnp.where(dev == tab[0:1, at], m, 0.0), axis=0, keepdims=True)
            for o in THREE:
                out[3 * t + o] = v[:, o * pair:(o + 1) * pair]
        loop(count, body)

    def issue(t):
        if t + 1 < CHUNKS:
            axis_first(t + 1, 1)
            axis_second(t + 1, 1)
        axis_first(t, 2)

    def visit1(t):
        if t >= 1:
            sides_in(t - 1)
            across_in(t - 1)
        if t + 2 < CHUNKS:
            p0_forward(t + 2)
        if t + 1 < CHUNKS:
            axis_forward(t + 1, 1)
        axis_second(t, 2)

    def visit2(t):
        axis_forward(t, 2)
        if t + 2 < CHUNKS:
            await_group(t + 2, 0, ACROSS)
        if t + 1 < CHUNKS:
            await_group(t + 1, 1, SECOND)
            await_group(t + 1, 1, ACROSS)
            if t + 3 in LATE:
                p0_send(t + 3)
            issue(t + 1)
        if t >= 1:
            await_siblings(t - 1, FIRST, SECOND, ACROSS)

    def load_cols(k, u, slot):
        x = u // 3
        c = lax.rem(u, 3)
        for s in range(2):
            g = (k * 2 + s) * 3 + c
            dst = wbuf.at[slot, :, :, :, pl.ds(s * lane, lane)]

            @pl.when(c == 0)
            def _():
                pltpu.make_async_copy(G12.at[g, :, :, x], dst, LS.at[slot]).start()

            @pl.when(c == 1)
            def _():
                pltpu.make_async_copy(G12.at[g, x], dst, LS.at[slot]).start()

            @pl.when(c > 1)
            def _():
                for y in range(4):
                    pltpu.make_async_copy(
                        G12.at[g, y, x], wbuf.at[slot, :, y, :, pl.ds(s * lane, lane)], LS.at[slot]).start()

    def load_rows(k, c, z, slot):
        for s in range(2):
            g = ((k - 6) * 2 + s) * 3 + c
            pltpu.make_async_copy(
                G3.at[g, z], wbuf3.at[slot, :, :, :, pl.ds(s * 3 * lane, 3 * lane)], LS.at[slot]).start()

    def run_units(load, k, body, lo=0, hi=UNITS):
        load(k, lo, lo % SLOTS)
        load(k, lo + 1, (lo + 1) % SLOTS)

        def step(u):
            slot = lax.rem(u, SLOTS)
            take(wbuf.at[slot], LS.at[slot])

            @pl.when(u + 2 < hi)
            def _():
                load(k, u + 2, lax.rem(u + 2, SLOTS))
            body(u, slot)
        loop(hi, step, lo)

    def weight(slot):
        return wbuf[slot].reshape(d, pair)

    def qkv_unit(k):
        def body(u, slot):
            p = 12 * k + u
            r = jnp.dot(h[...], weight(slot), preferred_element_type=F32) + bqkv[p]
            t = r.astype(BF).T
            row = pl.multiple_of(p * pair, pair)

            @pl.when(p < 9)
            def _():
                qt[pl.ds(row, pair), :] = t

            @pl.when(p >= 9)
            def _():
                kv_ref[pl.ds(pl.multiple_of(row - d, pair), pair), :] = t
        return body

    def out_unit(u, slot):
        p = u - 3
        cols = pl.ds(pl.multiple_of(p * pair, pair), pair)
        r = jnp.dot(ctx[...], weight(slot), preferred_element_type=F32)
        x1[:, cols] = (x_ref[:, cols].astype(F32) + r + bout[p]).astype(BF)

    def up_unit(k):
        def body(u, slot):
            p = 12 * (k - 3) + u
            cols = pl.ds(pl.multiple_of(p * pair, pair), pair)
            r = jnp.dot(h[...], weight(slot), preferred_element_type=F32) + bup[p]
            a[:, cols] = jax.nn.gelu(r, approximate=True).astype(BF)
        return body

    def run_down(k, lo=0, hi=UNITS):
        order = lambda o: jnp.where(o == 2, 3, jnp.where(o == 3, 2, o))
        n = 16 * (rows // 3)

        def split(u):
            c = lax.rem(u, 3)
            _, _, i2 = place(c)
            return c, wrap(i2 + order(u // 3))

        def load(u):
            c, z = split(u)
            load_rows(k, c, z, lax.rem(u, SLOTS))
        load(lo)
        load(lo + 1)

        def step(u):
            slot = lax.rem(u, SLOTS)
            take(wbuf3.at[slot], LS.at[slot])

            @pl.when(u + 2 < hi)
            def _():
                load(u + 2)
            c, z = split(u)
            at = pl.ds(pl.multiple_of((c * 4 + z) * n, lane), n)
            r = jnp.dot(a[:, at], wbuf3[slot].reshape(n, 6 * lane), preferred_element_type=F32)

            @pl.when(u == 0)
            def _():
                acc[...] = r

            @pl.when(u > 0)
            def _():
                acc[...] += r
        loop(hi, step, lo)
        if hi == UNITS:
            cols = slice((k - 6) * 6 * lane, (k - 5) * 6 * lane)
            y_ref[:, cols] = (x1[:, cols].astype(F32) + acc[...] + bdown[:, cols]).astype(BF)

    def norm(src, which):
        n = seq // 8

        def step(b):
            at = pl.ds(pl.multiple_of(b * n, n), n)
            v = src[at, :].astype(F32)
            v = v - jnp.mean(v, axis=-1, keepdims=True)
            var = jnp.mean(v * v, axis=-1, keepdims=True)
            h[at, :] = (v * lax.rsqrt(var + LN_EPS) * lnv[which] + lnv[which + 1]).astype(BF)
        loop(8, step)

    def attend(lo, hi):
        qb = seq // 2
        scale = hd ** -0.5

        def step(i):
            q_rows = pl.ds(pl.multiple_of(i * hd, hd), hd)
            k_rows = q_rows
            v_rows = pl.ds(pl.multiple_of(i * hd + d, hd), hd)
            for b in range(2):
                n = (b + 1) * qb
                q = qt[q_rows, b * qb:n]
                s = lax.dot_general(q, kv_ref[k_rows, :n], (((0,), (0,)), ((), ())),
                                    preferred_element_type=F32) * scale
                row = lax.broadcasted_iota(jnp.int32, (qb, n), 0) + b * qb
                col = lax.broadcasted_iota(jnp.int32, (qb, n), 1)
                s = jnp.where(col <= row, s, -jnp.inf)
                e = jnp.exp(s - jnp.max(s, axis=-1, keepdims=True))
                w = (e / jnp.sum(e, axis=-1, keepdims=True)).astype(BF)
                o = lax.dot_general(kv_ref[v_rows, :n], w, (((1,), (1,)), ((), ())),
                                    preferred_element_type=F32)
                ctxt[q_rows, b * qb:n] = o.astype(BF)
        loop(hi, step, lo)

    def flip():
        def step(i):
            at = pl.ds(pl.multiple_of(i * pair, pair), pair)
            ctx[:, at] = ctxt[at, :].T
        loop(d // pair, step)

    for k in THREE:
        x_send(k)
    v_send(0)
    x3_send()
    x_blocks(0)
    p0_send(0)
    for k in (1, 2):
        x_blocks(k)
        p0_send(k)
    p0_forward(0)
    x3_blocks()
    await_group(0, 0, ACROSS)
    axis_first(0, 1)
    axis_second(0, 1)
    p0_forward(1)
    p0_send(6)
    axis_forward(0, 1)
    p0_send(7)
    p0_send(8)
    await_group(1, 0, ACROSS)
    await_group(0, 1, SECOND)
    await_group(0, 1, ACROSS)
    issue(0)
    for k in LATE:
        x_send(k)
    v_send(1)
    visit1(0)
    v_send(2)
    for k in LATE:
        x_blocks(k)
    visit2(0)
    v_rows()
    norm(x_ref, 0)
    visit1(1)
    v_long(0, bqkv, d, 9)
    visit2(1)
    run_units(load_cols, 0, qkv_unit(0))
    visit1(2)
    v_long(1, bup, 4 * d, 12)
    visit2(2)
    run_units(load_cols, 1, qkv_unit(1))
    visit1(3)
    visit2(3)
    run_units(load_cols, 2, qkv_unit(2), hi=3)
    a1 = heads * 5 // 12
    a2 = heads * 9 // 12
    attend(0, a1)
    visit1(4)
    attend(a1, a2)
    visit2(4)
    attend(a2, heads)
    flip()
    run_units(load_cols, 2, out_unit, 3)
    visit1(5)
    norm(x1, 2)
    run_units(load_cols, 3, up_unit(3))
    visit2(5)
    run_units(load_cols, 4, up_unit(4))
    visit1(6)
    visit2(6)
    run_units(load_cols, 5, up_unit(5))
    visit1(7)
    visit2(7)
    run_down(6)
    visit1(8)
    visit2(8)
    run_down(7)
    await_siblings(8, FIRST)
    run_down(8, 0, 3)
    sides_in(8)
    await_siblings(8, SECOND)
    run_down(8, 3, 9)
    across_in(8)
    await_siblings(8, ACROSS)
    run_down(8, 9)

    for k in range(CHUNKS):
        ref = Block(k).ref
        for p in THREE:
            take(ref.at[(ALL3,) + ZEROS[:2 - p] + (ALL3,)], S.at[k, p])
        take(ref.at[ALL3], S.at[k, SIBLING])
    for k in range(6):
        take(stage12.at[pl.ds(0, 7), pl.ds(3 * k, 3)], XS.at[k])
    take(stage3.at[0], XS.at[6])
    take(V.at[0, 0, pl.ds(0, 7)], VS.at[0])
    take(V.at[0, ALL3], VS.at[1])
    take(V.at[ALL3], VS.at[2])


def solution(mesh):
    batch_axes = ('dp', 'fsdp')

    def local_layer(prompts, ln1_gain, ln1_bias, w_qkv, b_qkv, w_out, b_out, ln2_gain, ln2_bias, w_up, b_up, w_down, b_down):
        _, seq, d = prompts.shape
        heads, hd = w_qkv.shape[2], w_qkv.shape[3]
        lane = d // 18
        rows = d // 16
        pair = 2 * lane
        third = rows // 3
        r = w_up.shape[0]

        parts = [ln1_gain, ln1_bias, b_out, ln2_gain, ln2_bias, b_down, b_qkv, b_up]
        vec = jnp.stack([jnp.pad(p, (0, 128 - p.shape[0])) for p in parts]).astype(BF)

        orders = ((0, 1, 2), (2, 0, 1), (1, 2, 0))

        def reorder(m):
            m = m.reshape(-1, 4, 4, 4, 3, third)
            return [m[:, :, :, :, c].transpose((0,) + tuple(1 + o for o in orders[c]) + (4,)).reshape(m.shape[0], -1)
                    for c in THREE]

        w1 = jnp.concatenate([w_qkv.reshape(r, -1), w_out], axis=1)
        w2 = jnp.concatenate(reorder(w_up), axis=1)

        hidden = np.arange(4 * d).reshape(4, 4, 4, 3, third)
        hidden = np.concatenate([hidden[:, :, :, c].transpose(orders[c] + (3,)).reshape(-1) for c in THREE])
        index = [(np.arange(d), d // 128), (np.arange(3 * d), 3 * d // 128), (hidden, 4 * d // 128)]
        tab = np.stack([np.concatenate([i // n for i, n in index]), np.concatenate([i % n for i, n in index])])

        dims = (seq, d, heads, hd, rows, lane)
        vm = pl.BlockSpec(memory_space=pltpu.VMEM)
        hbm = pl.BlockSpec(memory_space=pl.ANY)
        dma = pltpu.SemaphoreType.DMA
        act, act_t = pltpu.VMEM((seq, d), BF), pltpu.VMEM((d, seq), BF)
        y, kv, _, _ = pl.pallas_call(
            functools.partial(layer_kernel, dims),
            out_shape=(
                pltpu.VMEM((seq, d), BF),
                pltpu.VMEM((2 * d, seq), BF),
                jax.ShapeDtypeStruct((36, 4, 4, 4, rows, lane), BF),
                jax.ShapeDtypeStruct((18, 4, 4, 4, third, 3 * lane), BF),
            ),
            in_specs=[vm] * 6,
            out_specs=(vm, vm, hbm, hbm),
            scratch_shapes=[
                act, act_t, act_t, act, act,
                pltpu.VMEM((seq, 4 * d), BF),
                pltpu.VMEM((SLOTS, 4, 4, rows, pair), BF),
                pltpu.VMEM((SLOTS, 4, 4, third, 6 * lane), BF),
                pltpu.VMEM((seq, 6 * lane), F32),
                pltpu.VMEM((18, rows, lane), BF),
                pltpu.VMEM((9, third, 3 * lane), BF),
                pltpu.VMEM((8, 18, r, lane), BF),
                pltpu.VMEM((2, 3, w_down.shape[0], 3 * lane), BF),
                pltpu.VMEM((4, 4, 8, 8, 128), BF),
                pltpu.VMEM((4, 1, d), F32),
                pltpu.VMEM((27, 1, pair), F32),
                pltpu.VMEM((9, 1, pair), F32),
                pltpu.VMEM((36, 1, pair), F32),
                pltpu.VMEM((1, d), F32),
                pltpu.VMEM((2, 128, 128), BF),
                dma((3 * CHUNKS, 4, 3)),
                dma((CHUNKS, 4)),
                dma((SLOTS,)),
                dma((CHUNKS,)),
                dma((7,)),
                dma((7,)),
                dma((3,)),
                dma((3,)),
            ],
            compiler_params=pltpu.CompilerParams(
                has_side_effects=True, vmem_limit_bytes=50 << 20),
            name="layer",
        )(prompts[0], w1, w2, w_down, vec, jnp.asarray(tab, jnp.int32))
        kc, vc = (m.reshape(heads, hd, seq).transpose(2, 0, 1)[None] for m in (kv[:d], kv[d:]))
        return y[None], kc, vc

    weight_spec = P('fsdp')
    return jax.shard_map(local_layer, mesh=mesh, in_specs=(P(batch_axes),) + (weight_spec,) * 12, out_specs=(P(batch_axes), P(batch_axes), P(batch_axes)), check_vma=False)
```

time: 522 us -> 314 us (0.60)
  Pallas kernels: 0 us -> 296 us
  waiting for transfers between devices: 215 us -> 0 us
  matrix products: 120 us -> 0 us
  blocking collectives: 71.4 us -> 0 us
  local copies, waits for them, and re-layouts: 73.9 us -> 15.9 us
  other arithmetic: 25.4 us -> 0.97 us
  between operations: 13.9 us -> 0.7 us
    pallas_call x0 -> x1, Pallas kernels: none -> 296 us  [local_layer(): pl.pallas_call(functools.partial(layer_kernel, dims), out_shape=(pltpu.VM...]
    all_gather x4 -> x0, waiting for transfers between devices: 212 us -> none  [gather_full(): return lax.all_gather(shard, 'fsdp', axis=0, tiled=True)]
    dot_general x8 -> x0, matrix products: 120 us -> none  [the longest x1 33.8 us: local_layer(): jnp.einsum('bsd,df->bsf', normed2, w_up_full, preferred_element_type=jnp....]
    unnamed x1 -> x0, blocking collectives: 71.4 us -> none
    unnamed x33 -> x3, local copies, waits for them, and re-layouts: 54.3 us -> 1.41 us
    sub x2 -> x0, other arithmetic: 17.6 us -> none  [one_block(): probs = jax.nn.softmax(scores, axis=-1).astype(jnp.bfloat16)]
    reshape x1 -> x4, local copies, waits for them, and re-layouts: 15.5 us -> 5.07 us  [the longest x1 2.91 us: reorder(): m = m.reshape(-1, 4, 4, 4, 3, third)]
    slice x0 -> x2, local copies, waits for them, and re-layouts: none -> 5.26 us  [the longest x1 2.77 us: reorder(): m[:, :, :, :, c].transpose((0,) + tuple((1 + o for o in orders[c])) + (4,))]
  transfers between devices with their start and end apart: 4 -> 0, of which waited for: 3 -> 0; matrix products, arithmetic and copies ran while one was open for 36% -> 0% of each run, Pallas kernels for 0% -> 0%
where the time goes in v2:
time: 314 us
  Pallas kernels  296 us (94%)
  local copies, waits for them, and re-layouts  15.9 us (5%)
    pallas_call x1, Pallas kernels, local_layer(): pl.pallas_call(functools.partial(layer_kernel, dims), out_shape=(pltpu.VM...  296 us

profile of v2, /device:TPU:1, one launch (start us, length us, event | category | flops | bytes accessed | tf_op | source)
XLA Modules:
  0.0 313.8 jit_solution(8058588145566581240)
XLA Ops:
  0.6 0.7 pad_bitcast_fusion.6
  1.3 0.7 pad_bitcast_fusion
  2.0 0.7 pad_bitcast_fusion.4
  2.7 0.7 pad_bitcast_fusion.2
  3.3 0.6 stack.35.vec
  3.9 1.3 reshape.24
  5.3 2.9 reshape.25
  8.2 2.8 slice_reduce_fusion
  11.0 0.0 copy-start
  11.0 0.4 reshape_squeeze.3
  11.4 0.2 copy.30
  11.6 0.4 reshape.27
  12.1 0.2 copy.31
  12.2 0.4 reshape.26
  12.7 0.0 copy-done
  12.7 1.0 pad_maximum_fusion
  13.6 296.3 %layer.1 = (bf16[512,2304]{1,0:T(8,128)(2,1)S(1)}, bf16[4608,512]{1,0:T(8,128)(2,1)S(1)}, bf16[36,4,4,4,144,128]{5,4,3,2,1,0:T(8,128)(2,1)}, bf16[18,4,4,4,48,384]{5,4,3,2,1,0:T(8,128)(2,1)}) custom-call(bf16[512,2304]{1,0:T(8,128)(2,1)} %bitcast.43, bf16[18,9216]{1,0:T(8,128)(2,1)} %get-tuple-element.20.w1, bf16[18,9216]{1,0:T(8,128)(2,1)} %get-tuple-element.21.w2, ...), custom_call_target="tpu_custom_call" | custom-call | tf_op jit(solution)/shard_map/layer/pallas_call | solution.py:570
  309.9 1.4 copy.33
  311.3 2.5 fusion
Async XLA Ops:
  11.0 1.7 copy-start

commit v3 on v2

--- a/solution.py
+++ b/solution.py
@@ -19,6 +19,8 @@
 ZEROS = (0, 0, 0)
 THREE = range(3)
 UNITS = 12
+QKV = 9
+LINE = 8
 LANES = 128
 LATE = (3, 4, 5)
 
@@ -34,10 +36,10 @@
     return lax.rem(i, 4)
 
 
-def layer_kernel(dims, x_ref, w1, w2, w3, vec, tab,
-                 y_ref, kv_ref, G12, G3,
-                 h, qt, ctxt, ctx, x1, a, wbuf, wbuf3, acc, own12, own3, stage12, stage3, V, lnv, bqkv, bout, bup, bdown, vrow,
-                 R, S, LS, OS, X, XS, VR, VS):
+def layer_kernel(dims, x_hbm, wq, wo, w2, w3, tab, *refs):
+    vecs, (y_ref, kv_ref, G12, G3), refs = refs[:8], refs[8:12], refs[12:]
+    (x_ref, h, qt, ctxt, ctx, x1, a, wbuf, wbuf3, acc, own12, own3, w2p, stage12, stage3, vec32, vec, V, lnv, bqkv, bout,
+     bup, bdown, vrow, R, S, LS, OS, X, XS, VR, VS) = refs
     seq, d, heads, hd, rows, lane = dims
     pair = 2 * lane
     me = lax.axis_index("fsdp")
@@ -46,7 +48,15 @@
     cy = wrap(me // 8)
     cz = me // 32
     sib = me + 1 - 2 * core
-    spot = lax.rem(me, 8)
+    spot = lax.rem(me, LINE)
+    line = [me - spot + lax.rem(spot + o, LINE) for o in range(1, LINE)]
+    column = [me + (wrap(cy + o) - cy) * 8 for o in range(1, 4)]
+    pillar = [me + (wrap(cz + o) - cz) * 32 for o in range(1, 4)]
+
+    barrier = pltpu.get_barrier_semaphore()
+    partners = line + column + pillar
+    for dev in partners:
+        pl.semaphore_signal(barrier, inc=1, device_id={"fsdp": dev}, device_id_type=MESH)
 
     class Block:
         def __init__(self, k):
@@ -175,55 +185,88 @@
         await_group(k, 2, ACROSS)
         colours(lambda c: to_sibling(k, c, 2, ACROSS))
 
-    def x_send(k):
-        src = w1 if k < 3 else w2
-        j = k % 3
-
-        def part(i, c):
-            tile = 24 * j + 6 * (i // 2) + 2 * c + lax.rem(i, 2)
-            return src.at[:, pl.ds(pl.multiple_of(tile * lane, lane), lane)]
-
-        def body(o):
-            i = lax.rem(spot + o, 8)
-            for c in THREE:
-                send(part(i, c), stage12.at[spot, 3 * k + c], XS.at[k], X.at[k], me - spot + i)
-        loop(8, body, 1)
+    share = QKV * lane
+
+    def x_send(m, lo, n):
+        at = stage12.at[m, spot, :, pl.ds(lo, n)]
+
+        def give(src, i, dev):
+            part = src.at[:, pl.ds(pl.multiple_of(i * share + lo, lane), n)]
+            sem = 2 * m + (lo > 0)
+            if dev is None:
+                pltpu.make_async_copy(part, at, X.at[sem]).start()
+            else:
+                send(part, at, XS.at[sem], X.at[sem], dev)
+
+        def route(i, dev):
+            if m:
+                give(w2p, i, dev)
+                return
+
+            @pl.when(i < 6)
+            def _():
+                give(wq, i, dev)
+
+            @pl.when(i >= 6)
+            def _():
+                give(wo, i - 6, dev)
+        for dev in line:
+            route(lax.rem(dev, LINE), dev)
+        route(spot, None)
+
+    def x_wait(m, lo, n):
+        take(stage12.at[m, :, :, pl.ds(lo, n)], X.at[2 * m + (lo > 0)])
+
+    def x_blocks(k):
         for c in THREE:
-            pltpu.make_async_copy(part(spot, c), stage12.at[spot, 3 * k + c], X.at[k]).start()
-
-    def x_blocks(k):
-        take(stage12.at[:, pl.ds(3 * k, 3)], X.at[k])
-        for c in THREE:
-            q = 3 * k + c
-            own12[q] = jnp.concatenate([stage12[i, q].astype(F32) for i in range(8)], axis=0).astype(BF)
+            lanes = pl.ds((3 * (k % 3) + c) * lane, lane)
+            own12[3 * k + c] = jnp.concatenate(
+                [stage12[k // 3, i, :, lanes].astype(F32) for i in range(LINE)], axis=0).astype(BF)
 
     def x3_send():
-        for j in THREE:
-            part = lambda s: w3.at[:, pl.ds(pl.multiple_of((2 * j + s) * 3 * lane, lane), 3 * lane)]
-            send(part(1 - core), stage3.at[core, j], XS.at[6], X.at[6], sib)
-            pltpu.make_async_copy(part(core), stage3.at[core, j], X.at[6]).start()
+        part = lambda s: w3.at[:, pl.ds(pl.multiple_of(s * share, lane), share)]
+        send(part(1 - core), stage3.at[core], XS.at[4], X.at[4], sib)
+        pltpu.make_async_copy(part(core), stage3.at[core], X.at[4]).start()
 
     def x3_blocks():
-        take(stage3, X.at[6])
+        take(stage3, X.at[4])
         n = rows // 3
         for j in THREE:
-            both = jnp.concatenate([stage3[0, j].astype(F32), stage3[1, j].astype(F32)], axis=0)
+            lanes = slice(3 * j * lane, 3 * (j + 1) * lane)
+            both = jnp.concatenate([stage3[s, :, lanes].astype(F32) for s in range(2)], axis=0)
             for c in THREE:
                 own3[3 * j + c] = both[c * n:(c + 1) * n].astype(BF)
 
+    def permute_up():
+        n = rows // 3
+        for c in THREE:
+            v = (1, 4, 16)
+            s0, s1, s2 = v[c:] + v[:c]
+            for i in range(4):
+                chips = [i * s2 + j * s1 + k * s0 for j in range(4) for k in range(4)]
+                groups = [w2[:, q * rows + c * n:q * rows + (c + 1) * n].astype(F32) for q in chips]
+                w2p[:, (4 * c + i) * 16 * n:(4 * c + i + 1) * 16 * n] = jnp.concatenate(groups, axis=1).astype(BF)
+
+    def v_pack():
+        vec32[...] = jnp.zeros_like(vec32)
+        for i, ref in enumerate(vecs):
+            vec32[i:i + 1, 0:ref.shape[1]] = ref[...].astype(F32)
+        vec[...] = vec32[...].astype(BF)
+
     def v_send(axis):
         if axis == 0:
-            for o in range(1, 8):
-                send(vec, V.at[cz, cy, spot], VS.at[0], VR.at[0], me - spot + lax.rem(spot + o, 8))
-            pltpu.make_async_copy(vec, V.at[cz, cy, spot], VR.at[0]).start()
+            part = V.at[cz, cy, spot]
+            for dev in line:
+                send(vec, part, VS.at[0], VR.at[0], dev)
+            pltpu.make_async_copy(vec, part, VR.at[0]).start()
         elif axis == 1:
             take(V.at[0, 0], VR.at[0])
-            for o in range(1, 4):
-                send(V.at[cz, cy], V.at[cz, cy], VS.at[1], VR.at[1], me + (wrap(cy + o) - cy) * 8)
+            for dev in column:
+                send(V.at[cz, cy], V.at[cz, cy], VS.at[1], VR.at[1], dev)
         else:
-            take(V.at[0, pl.ds(0, 3)], VR.at[1])
-            for o in range(1, 4):
-                send(V.at[cz], V.at[cz], VS.at[2], VR.at[2], me + (wrap(cz + o) - cz) * 32)
+            take(V.at[0, ALL3], VR.at[1])
+            for dev in pillar:
+                send(V.at[cz], V.at[cz], VS.at[2], VR.at[2], dev)
 
     def spread(vals, at):
         n = at.size
@@ -236,18 +279,19 @@
 
         def body(t):
             at = pl.ds(pl.multiple_of(t * pair, pair), pair)
-            m = spread(V[...].reshape(-1, LANES), at).reshape(LANES, 8, pair)
+            m = spread(V[...].reshape(-1, LANES), at).reshape(LANES, LINE, pair)
             dev = lax.broadcasted_iota(jnp.int32, m.shape, 0)
             v = jnp.sum(jnp.where(dev == tab[0:1, at][None], m, 0.0), axis=0)
             for i, src in enumerate((0, 1, 3, 4)):
                 lnv[i, :, at] = v[src:src + 1]
-            bout[t] = v[2:3]
+            for o in range(2):
+                bout[2 * t + o] = v[2:3, o * lane:(o + 1) * lane]
             bdown[:, at] = v[5:6]
         loop(nd, body)
-        dev = lax.broadcasted_iota(jnp.int32, (LANES, 8 * LANES), 0)
-        slot = lax.broadcasted_iota(jnp.int32, (LANES, 8 * LANES), 1)
+        dev = lax.broadcasted_iota(jnp.int32, (LANES, LINE * LANES), 0)
+        slot = lax.broadcasted_iota(jnp.int32, (LANES, LINE * LANES), 1)
         for i in range(2):
-            take_row = (slot == dev * 8 + 6 + i).astype(BF)
+            take_row = (slot == dev * LINE + 6 + i).astype(BF)
             vrow[i] = jnp.dot(take_row, V[...].reshape(-1, LANES), preferred_element_type=F32).astype(BF)
 
     def v_long(i, out, first, count):
@@ -258,8 +302,8 @@
             m = spread(vrow[i], at)
             dev = lax.broadcasted_iota(jnp.int32, m.shape, 0)
             v = jnp.sum(jnp.where(dev == tab[0:1, at], m, 0.0), axis=0, keepdims=True)
-            for o in THREE:
-                out[3 * t + o] = v[:, o * pair:(o + 1) * pair]
+            for o in range(6):
+                out[6 * t + o] = v[:, o * lane:(o + 1) * lane]
         loop(count, body)
 
     def issue(t):
@@ -269,27 +313,29 @@
         axis_first(t, 2)
 
     def visit1(t):
-        if t >= 1:
-            sides_in(t - 1)
-            across_in(t - 1)
-        if t + 2 < CHUNKS:
-            p0_forward(t + 2)
-        if t + 1 < CHUNKS:
-            axis_forward(t + 1, 1)
+        last, ahead, far = t - 1, t + 1, t + 2
+        if t:
+            sides_in(last)
+            across_in(last)
+        if far < CHUNKS:
+            p0_forward(far)
+        if ahead < CHUNKS:
+            axis_forward(ahead, 1)
         axis_second(t, 2)
 
     def visit2(t):
+        last, ahead, far, farther = t - 1, t + 1, t + 2, t + 3
         axis_forward(t, 2)
-        if t + 2 < CHUNKS:
-            await_group(t + 2, 0, ACROSS)
-        if t + 1 < CHUNKS:
-            await_group(t + 1, 1, SECOND)
-            await_group(t + 1, 1, ACROSS)
-            if t + 3 in LATE:
-                p0_send(t + 3)
-            issue(t + 1)
-        if t >= 1:
-            await_siblings(t - 1, FIRST, SECOND, ACROSS)
+        if far < CHUNKS:
+            await_group(far, 0, ACROSS)
+        if ahead < CHUNKS:
+            for role in (SECOND, ACROSS):
+                await_group(ahead, 1, role)
+            if farther in LATE:
+                p0_send(farther)
+            issue(ahead)
+        if t:
+            await_siblings(last, FIRST, SECOND, ACROSS)
 
     def load_cols(k, u, slot):
         x = u // 3
@@ -335,34 +381,43 @@
     def weight(slot):
         return wbuf[slot].reshape(d, pair)
 
+    def tiles(k, u):
+        first = 18 * (u // 3) + 3 * (k % 3) + lax.rem(u, 3)
+        return first, first + QKV
+
+    def span(t):
+        return pl.ds(pl.multiple_of(t * lane, lane), lane)
+
+    def both(r):
+        return r[:, :lane], r[:, lane:]
+
     def qkv_unit(k):
         def body(u, slot):
-            p = 12 * k + u
-            r = jnp.dot(h[...], weight(slot), preferred_element_type=F32) + bqkv[p]
-            t = r.astype(BF).T
-            row = pl.multiple_of(p * pair, pair)
-
-            @pl.when(p < 9)
-            def _():
-                qt[pl.ds(row, pair), :] = t
-
-            @pl.when(p >= 9)
-            def _():
-                kv_ref[pl.ds(pl.multiple_of(row - d, pair), pair), :] = t
+            r = jnp.dot(h[...], weight(slot), preferred_element_type=F32)
+            for t, v in zip(tiles(k, u), both(r)):
+                v = (v + bqkv[t]).astype(BF).T
+
+                @pl.when(t < 18)
+                def _():
+                    qt[span(t), :] = v
+
+                @pl.when(t >= 18)
+                def _():
+                    kv_ref[span(t - 18), :] = v
         return body
 
-    def out_unit(u, slot):
-        p = u - 3
-        cols = pl.ds(pl.multiple_of(p * pair, pair), pair)
-        r = jnp.dot(ctx[...], weight(slot), preferred_element_type=F32)
-        x1[:, cols] = (x_ref[:, cols].astype(F32) + r + bout[p]).astype(BF)
+    def out_unit(k):
+        def body(u, slot):
+            r = jnp.dot(ctx[...], weight(slot), preferred_element_type=F32)
+            for t, v in zip(tiles(k, u - QKV), both(r)):
+                x1[:, span(t)] = (x_ref[:, span(t)].astype(F32) + v + bout[t]).astype(BF)
+        return body
 
     def up_unit(k):
         def body(u, slot):
-            p = 12 * (k - 3) + u
-            cols = pl.ds(pl.multiple_of(p * pair, pair), pair)
-            r = jnp.dot(h[...], weight(slot), preferred_element_type=F32) + bup[p]
-            a[:, cols] = jax.nn.gelu(r, approximate=True).astype(BF)
+            r = jnp.dot(h[...], weight(slot), preferred_element_type=F32)
+            for t, v in zip(tiles(k, u), both(r)):
+                a[:, span(t)] = jax.nn.gelu(v + bup[t], approximate=True).astype(BF)
         return body
 
     def run_down(k, lo=0, hi=UNITS):
@@ -400,8 +455,10 @@
                 acc[...] += r
         loop(hi, step, lo)
         if hi == UNITS:
-            cols = slice((k - 6) * 6 * lane, (k - 5) * 6 * lane)
-            y_ref[:, cols] = (x1[:, cols].astype(F32) + acc[...] + bdown[:, cols]).astype(BF)
+            n = 3 * lane
+            for s in range(2):
+                cols = pl.ds(s * share + (k - 6) * n, n)
+                y_ref[:, cols] = (x1[:, cols].astype(F32) + acc[:, s * n:(s + 1) * n] + bdown[:, cols]).astype(BF)
 
     def norm(src, which):
         n = seq // 8
@@ -443,12 +500,19 @@
             ctx[:, at] = ctxt[at, :].T
         loop(d // pair, step)
 
-    for k in THREE:
-        x_send(k)
+    x_copy = pltpu.make_async_copy(x_hbm, x_ref, OS.at[CHUNKS])
+    x_copy.start()
+    v_pack()
+    pl.semaphore_wait(barrier, len(partners))
+    early, rest, whole = (0, 3 * lane), (3 * lane, 6 * lane), (0, share)
+    x_send(0, *early)
+    x_send(0, *rest)
+    x3_send()
     v_send(0)
-    x3_send()
+    x_wait(0, *early)
     x_blocks(0)
     p0_send(0)
+    x_wait(0, *rest)
     for k in (1, 2):
         x_blocks(k)
         p0_send(k)
@@ -466,11 +530,13 @@
     await_group(0, 1, SECOND)
     await_group(0, 1, ACROSS)
     issue(0)
-    for k in LATE:
-        x_send(k)
+    permute_up()
     v_send(1)
     visit1(0)
+    x_send(1, *whole)
     v_send(2)
+    x_copy.wait()
+    x_wait(1, *whole)
     for k in LATE:
         x_blocks(k)
     visit2(0)
@@ -479,23 +545,24 @@
     visit1(1)
     v_long(0, bqkv, d, 9)
     visit2(1)
-    run_units(load_cols, 0, qkv_unit(0))
+    run_units(load_cols, 0, qkv_unit(0), hi=QKV)
     visit1(2)
     v_long(1, bup, 4 * d, 12)
     visit2(2)
-    run_units(load_cols, 1, qkv_unit(1))
+    run_units(load_cols, 1, qkv_unit(1), hi=QKV)
     visit1(3)
     visit2(3)
-    run_units(load_cols, 2, qkv_unit(2), hi=3)
-    a1 = heads * 5 // 12
-    a2 = heads * 9 // 12
+    run_units(load_cols, 2, qkv_unit(2), hi=QKV)
+    a1 = heads * 5 // UNITS
+    a2 = heads * QKV // UNITS
     attend(0, a1)
     visit1(4)
     attend(a1, a2)
     visit2(4)
     attend(a2, heads)
     flip()
-    run_units(load_cols, 2, out_unit, 3)
+    for k in THREE:
+        run_units(load_cols, k, out_unit(k), QKV)
     visit1(5)
     norm(x1, 2)
     run_units(load_cols, 3, up_unit(3))
@@ -524,9 +591,9 @@
         for p in THREE:
             take(ref.at[(ALL3,) + ZEROS[:2 - p] + (ALL3,)], S.at[k, p])
         take(ref.at[ALL3], S.at[k, SIBLING])
-    for k in range(6):
-        take(stage12.at[pl.ds(0, 7), pl.ds(3 * k, 3)], XS.at[k])
-    take(stage3.at[0], XS.at[6])
+    for m, lo, n in ((0,) + early, (0,) + rest, (1,) + whole):
+        take(stage12.at[m, pl.ds(0, 7), :, pl.ds(lo, n)], XS.at[2 * m + (lo > 0)])
+    take(stage3.at[0], XS.at[4])
     take(V.at[0, 0, pl.ds(0, 7)], VS.at[0])
     take(V.at[0, ALL3], VS.at[1])
     take(V.at[ALL3], VS.at[2])
@@ -545,17 +612,7 @@
         r = w_up.shape[0]
 
         parts = [ln1_gain, ln1_bias, b_out, ln2_gain, ln2_bias, b_down, b_qkv, b_up]
-        vec = jnp.stack([jnp.pad(p, (0, 128 - p.shape[0])) for p in parts]).astype(BF)
-
         orders = ((0, 1, 2), (2, 0, 1), (1, 2, 0))
-
-        def reorder(m):
-            m = m.reshape(-1, 4, 4, 4, 3, third)
-            return [m[:, :, :, :, c].transpose((0,) + tuple(1 + o for o in orders[c]) + (4,)).reshape(m.shape[0], -1)
-                    for c in THREE]
-
-        w1 = jnp.concatenate([w_qkv.reshape(r, -1), w_out], axis=1)
-        w2 = jnp.concatenate(reorder(w_up), axis=1)
 
         hidden = np.arange(4 * d).reshape(4, 4, 4, 3, third)
         hidden = np.concatenate([hidden[:, :, :, c].transpose(orders[c] + (3,)).reshape(-1) for c in THREE])
@@ -575,38 +632,41 @@
                 jax.ShapeDtypeStruct((36, 4, 4, 4, rows, lane), BF),
                 jax.ShapeDtypeStruct((18, 4, 4, 4, third, 3 * lane), BF),
             ),
-            in_specs=[vm] * 6,
+            in_specs=[hbm] + [vm] * 13,
             out_specs=(vm, vm, hbm, hbm),
             scratch_shapes=[
-                act, act_t, act_t, act, act,
+                act, act, act_t, act_t, act, act,
                 pltpu.VMEM((seq, 4 * d), BF),
                 pltpu.VMEM((SLOTS, 4, 4, rows, pair), BF),
                 pltpu.VMEM((SLOTS, 4, 4, third, 6 * lane), BF),
                 pltpu.VMEM((seq, 6 * lane), F32),
                 pltpu.VMEM((18, rows, lane), BF),
                 pltpu.VMEM((9, third, 3 * lane), BF),
-                pltpu.VMEM((8, 18, r, lane), BF),
-                pltpu.VMEM((2, 3, w_down.shape[0], 3 * lane), BF),
-                pltpu.VMEM((4, 4, 8, 8, 128), BF),
+                pltpu.VMEM((r, 4 * d), BF),
+                pltpu.VMEM((2, LINE, r, QKV * lane), BF),
+                pltpu.VMEM((2, w_down.shape[0], QKV * lane), BF),
+                pltpu.VMEM((LINE, LANES), F32),
+                pltpu.VMEM((LINE, LANES), BF),
+                pltpu.VMEM((4, 4, LINE, LINE, LANES), BF),
                 pltpu.VMEM((4, 1, d), F32),
-                pltpu.VMEM((27, 1, pair), F32),
-                pltpu.VMEM((9, 1, pair), F32),
-                pltpu.VMEM((36, 1, pair), F32),
+                pltpu.VMEM((54, 1, lane), F32),
+                pltpu.VMEM((18, 1, lane), F32),
+                pltpu.VMEM((72, 1, lane), F32),
                 pltpu.VMEM((1, d), F32),
-                pltpu.VMEM((2, 128, 128), BF),
+                pltpu.VMEM((2, LANES, LANES), BF),
                 dma((3 * CHUNKS, 4, 3)),
                 dma((CHUNKS, 4)),
                 dma((SLOTS,)),
-                dma((CHUNKS,)),
-                dma((7,)),
-                dma((7,)),
+                dma((CHUNKS + 1,)),
+                dma((5,)),
+                dma((5,)),
                 dma((3,)),
                 dma((3,)),
             ],
             compiler_params=pltpu.CompilerParams(
-                has_side_effects=True, vmem_limit_bytes=50 << 20),
+                has_side_effects=True, collective_id=0, vmem_limit_bytes=50 << 20),
             name="layer",
-        )(prompts[0], w1, w2, w_down, vec, jnp.asarray(tab, jnp.int32))
+        )(prompts[0], w_qkv.reshape(r, -1), w_out, w_up, w_down, jnp.asarray(tab, jnp.int32), *(p[None] for p in parts))
         kc, vc = (m.reshape(heads, hd, seq).transpose(2, 0, 1)[None] for m in (kv[:d], kv[d:]))
         return y[None], kc, vc
 

time: 314 us -> 307 us (0.978)
  local copies, waits for them, and re-layouts: 15.9 us -> 5.95 us
  Pallas kernels: 296 us -> 300 us
    another operation x6 -> x0, local copies, waits for them, and re-layouts: 3.73 us -> none  [the longest x5 3.31 us: local_layer(): jnp.stack([jnp.pad(p, (0, 128 - p.shape[0])) for p in parts]).astype(BF)]
    pallas_call x1, Pallas kernels: 296 us -> 300 us  [local_layer(): pl.pallas_call(functools.partial(layer_kernel, dims), out_shape=(pltpu.VM...]
where the time goes in v3:
time: 307 us; the launch traced here: 306 us
  Pallas kernels  300 us (98%)
  local copies, waits for them, and re-layouts  5.95 us (2%)
    pallas_call x1, Pallas kernels, local_layer(): pl.pallas_call(functools.partial(layer_kernel, dims), out_shape=(pltpu.VM...  300 us

profile of v3, /device:TPU:1, one launch (start us, length us, event | category | flops | bytes accessed | tf_op | source)
XLA Modules:
  0.0 306.2 jit_solution(7626859458317413991)
XLA Ops:
  0.6 2.1 reshape.15.wq
  2.7 299.6 %layer.1 = (bf16[512,2304]{1,0:T(8,128)(2,1)S(1)}, bf16[4608,512]{1,0:T(8,128)(2,1)S(1)}, bf16[36,4,4,4,144,128]{5,4,3,2,1,0:T(8,128)(2,1)}, bf16[18,4,4,4,48,384]{5,4,3,2,1,0:T(8,128)(2,1)}) custom-call(bf16[512,2304]{1,0:T(8,128)(2,1)} %bitcast.23, bf16[18,6912]{1,0:T(8,128)(2,1)} %reshape.15.wq, bf16[18,2304]{1,0:T(8,128)(2,1)} %wo.1, ...), custom_call_target="tpu_custom_call" | custom-call | tf_op jit(solution)/shard_map/layer/pallas_call | solution.py:627
  302.3 1.4 copy.18
  303.7 2.5 fusion

commit v4 on v3

--- a/solution.py
+++ b/solution.py
@@ -503,6 +503,7 @@
     x_copy = pltpu.make_async_copy(x_hbm, x_ref, OS.at[CHUNKS])
     x_copy.start()
     v_pack()
+    permute_up()
     pl.semaphore_wait(barrier, len(partners))
     early, rest, whole = (0, 3 * lane), (3 * lane, 6 * lane), (0, share)
     x_send(0, *early)
@@ -524,17 +525,18 @@
     p0_forward(1)
     p0_send(6)
     axis_forward(0, 1)
+    await_group(1, 0, ACROSS)
+    axis_first(1, 1)
+    axis_second(1, 1)
+    x_send(1, *whole)
+    v_send(1)
     p0_send(7)
     p0_send(8)
-    await_group(1, 0, ACROSS)
     await_group(0, 1, SECOND)
     await_group(0, 1, ACROSS)
-    issue(0)
-    permute_up()
-    v_send(1)
+    axis_first(0, 2)
+    v_send(2)
     visit1(0)
-    x_send(1, *whole)
-    v_send(2)
     x_copy.wait()
     x_wait(1, *whole)
     for k in LATE:

time: 307 us -> 303 us (0.987)
  Pallas kernels: 300 us -> 296 us
    pallas_call x1, Pallas kernels: 300 us -> 296 us  [local_layer(): pl.pallas_call(functools.partial(layer_kernel, dims), out_shape=(pltpu.VM...]
where the time goes in v4:
time: 303 us
  Pallas kernels  296 us (98%)
  local copies, waits for them, and re-layouts  5.95 us (2%)
    pallas_call x1, Pallas kernels, local_layer(): pl.pallas_call(functools.partial(layer_kernel, dims), out_shape=(pltpu.VM...  296 us

profile of v4, /device:TPU:1, one launch (start us, length us, event | category | flops | bytes accessed | tf_op | source)
XLA Modules:
  0.0 302.6 jit_solution(3295685007911428486)
XLA Ops:
  0.6 2.1 reshape.15.wq
  2.7 296.0 %layer.1 = (bf16[512,2304]{1,0:T(8,128)(2,1)S(1)}, bf16[4608,512]{1,0:T(8,128)(2,1)S(1)}, bf16[36,4,4,4,144,128]{5,4,3,2,1,0:T(8,128)(2,1)}, bf16[18,4,4,4,48,384]{5,4,3,2,1,0:T(8,128)(2,1)}) custom-call(bf16[512,2304]{1,0:T(8,128)(2,1)} %bitcast.23, bf16[18,6912]{1,0:T(8,128)(2,1)} %reshape.15.wq, bf16[18,2304]{1,0:T(8,128)(2,1)} %wo.1, ...), custom_call_target="tpu_custom_call" | custom-call | tf_op jit(solution)/shard_map/layer/pallas_call | solution.py:629
  298.7 1.4 copy.18
  300.1 2.5 fusion

commit v5 on v4

--- a/solution.py
+++ b/solution.py
@@ -21,6 +21,9 @@
 UNITS = 12
 QKV = 9
 LINE = 8
+SIDES = (1, 3)
+QUARTERS = (0, *SIDES, ACROSS)
+LAST = CHUNKS - 1
 LANES = 128
 LATE = (3, 4, 5)
 
@@ -104,11 +107,10 @@
             take(B.ref.at[at], R.at[k * 3 + c, p, role])
         colours(body)
 
-    def await_siblings(k, *roles):
-        for role in roles:
-            B = Block(k)
-            part = LO if role == SECOND else 0
-            colours(lambda c: take(B.ref.at[B.slab(c), part], R.at[k * 3 + c, SIBLING, role]))
+    def await_siblings(k, *quarters):
+        B = Block(k)
+        for ahead in quarters:
+            colours(lambda c: take(B.ref.at[B.slab(c), 0], R.at[k * 3 + c, SIBLING, ahead]))
 
     def p0_send(k):
         B = Block(k)
@@ -140,10 +142,10 @@
         at = (B.slab(c), place(c)[2], i) if p == 1 else (B.slab(c), i)
         return B.ref.at[at + (LO,)], B.ref.at[at + (HI,)]
 
-    def to_sibling(k, c, ahead, role):
+    def to_sibling(k, c, ahead):
         B = Block(k)
         part = B.ref.at[B.slab(c), wrap(place(c)[2] + ahead)]
-        send(part, part, S.at[k, SIBLING], R.at[k * 3 + c, SIBLING, role], sib)
+        send(part, part, S.at[k, SIBLING], R.at[k * 3 + c, SIBLING, ahead], sib)
 
     def axis_first(k, p):
         def body(c):
@@ -152,7 +154,7 @@
             send(lo, lo, S.at[k, p], R.at[k * 3 + c, p, FIRST], right)
             send(hi, hi, S.at[k, p], R.at[k * 3 + c, p, FIRST], left)
             if p == 2:
-                to_sibling(k, c, 0, FIRST)
+                to_sibling(k, c, 0)
         colours(body)
 
     def axis_second(k, p):
@@ -176,14 +178,12 @@
     def sides_in(k):
         await_group(k, 2, SECOND)
 
-        def body(c):
-            to_sibling(k, c, 1, SECOND)
-            to_sibling(k, c, 3, SECOND)
-        colours(body)
+        for ahead in SIDES:
+            colours(lambda c: to_sibling(k, c, ahead))
 
     def across_in(k):
         await_group(k, 2, ACROSS)
-        colours(lambda c: to_sibling(k, c, 2, ACROSS))
+        colours(lambda c: to_sibling(k, c, ACROSS))
 
     share = QKV * lane
 
@@ -315,13 +315,15 @@
     def visit1(t):
         last, ahead, far = t - 1, t + 1, t + 2
         if t:
-            sides_in(last)
+            if t < LAST:
+                sides_in(last)
             across_in(last)
         if far < CHUNKS:
             p0_forward(far)
         if ahead < CHUNKS:
             axis_forward(ahead, 1)
-        axis_second(t, 2)
+        if t < LAST:
+            axis_second(t, 2)
 
     def visit2(t):
         last, ahead, far, farther = t - 1, t + 1, t + 2, t + 3
@@ -334,8 +336,12 @@
             if farther in LATE:
                 p0_send(farther)
             issue(ahead)
-        if t:
-            await_siblings(last, FIRST, SECOND, ACROSS)
+        if ahead == LAST:
+            axis_second(LAST, 2)
+        if t == LAST:
+            await_siblings(last, ACROSS)
+        elif t:
+            await_siblings(last, *QUARTERS)
 
     def load_cols(k, u, slot):
         x = u // 3
@@ -420,7 +426,7 @@
                 a[:, span(t)] = jax.nn.gelu(v + bup[t], approximate=True).astype(BF)
         return body
 
-    def run_down(k, lo=0, hi=UNITS):
+    def run_down(k, lo=0, hi=UNITS, known=UNITS, primed=False):
         order = lambda o: jnp.where(o == 2, 3, jnp.where(o == 3, 2, o))
         n = 16 * (rows // 3)
 
@@ -432,14 +438,15 @@
         def load(u):
             c, z = split(u)
             load_rows(k, c, z, lax.rem(u, SLOTS))
-        load(lo)
-        load(lo + 1)
+        if not primed:
+            load(lo)
+            load(lo + 1)
 
         def step(u):
             slot = lax.rem(u, SLOTS)
             take(wbuf3.at[slot], LS.at[slot])
 
-            @pl.when(u + 2 < hi)
+            @pl.when(u + 2 < known)
             def _():
                 load(u + 2)
             c, z = split(u)
@@ -575,18 +582,26 @@
     run_units(load_cols, 5, up_unit(5))
     visit1(7)
     visit2(7)
-    run_down(6)
-    visit1(8)
-    visit2(8)
-    run_down(7)
-    await_siblings(8, FIRST)
-    run_down(8, 0, 3)
-    sides_in(8)
-    await_siblings(8, SECOND)
-    run_down(8, 3, 9)
-    across_in(8)
-    await_siblings(8, ACROSS)
-    run_down(8, 9)
+    q1, q2, q3 = 3, 6, QKV
+    run_down(6, hi=q2)
+    sides_in(7)
+    run_down(6, q2, primed=True)
+    await_siblings(7, 0, *SIDES)
+    run_down(7, hi=q2, known=q3)
+    visit1(LAST)
+    run_down(7, q2, q3, q3, True)
+    visit2(LAST)
+    run_down(7, q3)
+    await_siblings(LAST, 0)
+    run_down(LAST, hi=q1, known=q1)
+    sides_in(LAST)
+    await_siblings(LAST, SIDES[0])
+    run_down(LAST, q1, q2, q2)
+    across_in(LAST)
+    await_siblings(LAST, SIDES[1])
+    run_down(LAST, q2, q3, q3)
+    await_siblings(LAST, ACROSS)
+    run_down(LAST, q3)
 
     for k in range(CHUNKS):
         ref = Block(k).ref
@@ -656,7 +671,7 @@
                 pltpu.VMEM((72, 1, lane), F32),
                 pltpu.VMEM((1, d), F32),
                 pltpu.VMEM((2, LANES, LANES), BF),
-                dma((3 * CHUNKS, 4, 3)),
+                dma((3 * CHUNKS, 4, 4)),
                 dma((CHUNKS, 4)),
                 dma((SLOTS,)),
                 dma((CHUNKS + 1,)),

time: 303 us -> 293 us (0.967)
  Pallas kernels: 296 us -> 286 us
    pallas_call x1, Pallas kernels: 296 us -> 286 us  [local_layer(): pl.pallas_call(functools.partial(layer_kernel, dims), out_shape=(pltpu.VM...]
where the time goes in v5:
time: 293 us; the launch traced here: 292 us
  Pallas kernels  286 us (98%)
  local copies, waits for them, and re-layouts  5.95 us (2%)
    pallas_call x1, Pallas kernels, local_layer(): pl.pallas_call(functools.partial(layer_kernel, dims), out_shape=(pltpu.VM...  286 us

profile of v5, /device:TPU:1, one launch (start us, length us, event | category | flops | bytes accessed | tf_op | source)
XLA Modules:
  0.0 292.2 jit_solution(9005609661813773327)
XLA Ops:
  0.6 2.1 reshape.15.wq
  2.7 285.6 %layer.1 = (bf16[512,2304]{1,0:T(8,128)(2,1)S(1)}, bf16[4608,512]{1,0:T(8,128)(2,1)S(1)}, bf16[36,4,4,4,144,128]{5,4,3,2,1,0:T(8,128)(2,1)}, bf16[18,4,4,4,48,384]{5,4,3,2,1,0:T(8,128)(2,1)}) custom-call(bf16[512,2304]{1,0:T(8,128)(2,1)} %bitcast.23, bf16[18,6912]{1,0:T(8,128)(2,1)} %reshape.15.wq, bf16[18,2304]{1,0:T(8,128)(2,1)} %wo.1, ...), custom_call_target="tpu_custom_call" | custom-call | tf_op jit(solution)/shard_map/layer/pallas_call | solution.py:644
  288.3 1.4 copy.18
  289.7 2.5 fusion

commit v6 on v5

--- a/solution.py
+++ b/solution.py
@@ -18,6 +18,8 @@
 FIRST, SECOND, ACROSS, SIBLING = range(4)
 ZEROS = (0, 0, 0)
 THREE = range(3)
+TWO = range(2)
+OTHERS = pl.ds(0, 7)
 UNITS = 12
 QKV = 9
 LINE = 8
@@ -39,9 +41,13 @@
     return lax.rem(i, 4)
 
 
+def thirds(u):
+    return u // 3, lax.rem(u, 3)
+
+
 def layer_kernel(dims, x_hbm, wq, wo, w2, w3, tab, *refs):
     vecs, (y_ref, kv_ref, G12, G3), refs = refs[:8], refs[8:12], refs[12:]
-    (x_ref, h, qt, ctxt, ctx, x1, a, wbuf, wbuf3, acc, own12, own3, w2p, stage12, stage3, vec32, vec, V, lnv, bqkv, bout,
+    (x_ref, h, qt, ctxt, ctx, x1, a, wbuf, wbuf3, acc, own12, own3, G8, w2p, stage12, stage3, vec32, vec, V, lnv, bqkv, bout,
      bup, bdown, vrow, R, S, LS, OS, X, XS, VR, VS) = refs
     seq, d, heads, hd, rows, lane = dims
     pair = 2 * lane
@@ -63,14 +69,16 @@
 
     class Block:
         def __init__(self, k):
-            self.ref = G12 if k < 6 else G3
-            self.base = k if k < 6 else k - 6
+            self.ref, self.base = (G12, k) if k < 6 else (G3, k - 6)
+            self.blocks, self.first = (own12, 3 * k) if k < 6 else (own3, 3 * (k - 6))
+            if k == LAST:
+                self.ref, self.base = G8, 0
 
         def slab(self, c):
             return (self.base * 2 + core) * 3 + c
 
         def own(self, c):
-            return (own12 if self.ref is G12 else own3).at[self.base * 3 + c]
+            return self.blocks.at[self.first + c]
 
     def pick(c, v):
         return jnp.where(c == 0, v[0], jnp.where(c == 1, v[1], v[2]))
@@ -233,7 +241,7 @@
         n = rows // 3
         for j in THREE:
             lanes = slice(3 * j * lane, 3 * (j + 1) * lane)
-            both = jnp.concatenate([stage3[s, :, lanes].astype(F32) for s in range(2)], axis=0)
+            both = jnp.concatenate([stage3[s, :, lanes].astype(F32) for s in TWO], axis=0)
             for c in THREE:
                 own3[3 * j + c] = both[c * n:(c + 1) * n].astype(BF)
 
@@ -250,7 +258,7 @@
     def v_pack():
         vec32[...] = jnp.zeros_like(vec32)
         for i, ref in enumerate(vecs):
-            vec32[i:i + 1, 0:ref.shape[1]] = ref[...].astype(F32)
+            vec32[i:i + 1, :ref.shape[1]] = ref[...].astype(F32)
         vec[...] = vec32[...].astype(BF)
 
     def v_send(axis):
@@ -284,13 +292,13 @@
             v = jnp.sum(jnp.where(dev == tab[0:1, at][None], m, 0.0), axis=0)
             for i, src in enumerate((0, 1, 3, 4)):
                 lnv[i, :, at] = v[src:src + 1]
-            for o in range(2):
+            for o in TWO:
                 bout[2 * t + o] = v[2:3, o * lane:(o + 1) * lane]
             bdown[:, at] = v[5:6]
         loop(nd, body)
         dev = lax.broadcasted_iota(jnp.int32, (LANES, LINE * LANES), 0)
         slot = lax.broadcasted_iota(jnp.int32, (LANES, LINE * LANES), 1)
-        for i in range(2):
+        for i in TWO:
             take_row = (slot == dev * LINE + 6 + i).astype(BF)
             vrow[i] = jnp.dot(take_row, V[...].reshape(-1, LANES), preferred_element_type=F32).astype(BF)
 
@@ -344,9 +352,8 @@
             await_siblings(last, *QUARTERS)
 
     def load_cols(k, u, slot):
-        x = u // 3
-        c = lax.rem(u, 3)
-        for s in range(2):
+        x, c = thirds(u)
+        for s in TWO:
             g = (k * 2 + s) * 3 + c
             dst = wbuf.at[slot, :, :, :, pl.ds(s * lane, lane)]
 
@@ -365,20 +372,22 @@
                         G12.at[g, y, x], wbuf.at[slot, :, y, :, pl.ds(s * lane, lane)], LS.at[slot]).start()
 
     def load_rows(k, c, z, slot):
-        for s in range(2):
+        for s in TWO:
             g = ((k - 6) * 2 + s) * 3 + c
             pltpu.make_async_copy(
                 G3.at[g, z], wbuf3.at[slot, :, :, :, pl.ds(s * 3 * lane, 3 * lane)], LS.at[slot]).start()
 
-    def run_units(load, k, body, lo=0, hi=UNITS):
-        load(k, lo, lo % SLOTS)
-        load(k, lo + 1, (lo + 1) % SLOTS)
+    def run_units(k, unit, lo=0, hi=UNITS, known=None, primed=False):
+        load, known, body = load_cols, known or hi, unit(k)
+        if not primed:
+            load(k, lo, lo % SLOTS)
+            load(k, lo + 1, (lo + 1) % SLOTS)
 
         def step(u):
             slot = lax.rem(u, SLOTS)
             take(wbuf.at[slot], LS.at[slot])
 
-            @pl.when(u + 2 < hi)
+            @pl.when(u + 2 < known)
             def _():
                 load(k, u + 2, lax.rem(u + 2, SLOTS))
             body(u, slot)
@@ -388,7 +397,8 @@
         return wbuf[slot].reshape(d, pair)
 
     def tiles(k, u):
-        first = 18 * (u // 3) + 3 * (k % 3) + lax.rem(u, 3)
+        x, c = thirds(u)
+        first = 18 * x + 3 * (k % 3) + c
         return first, first + QKV
 
     def span(t):
@@ -426,17 +436,32 @@
                 a[:, span(t)] = jax.nn.gelu(v + bup[t], approximate=True).astype(BF)
         return body
 
+    def quarter(u):
+        o, c = thirds(u)
+        return c, wrap(place(c)[2] + o + o // 2 - o // 3 * 2)
+
+    def down_lhs(c, z):
+        n = 16 * (rows // 3)
+        return a[:, pl.ds(pl.multiple_of((c * 4 + z) * n, lane), n)]
+
+    def add(u, cols, r):
+        @pl.when(u == 0)
+        def _():
+            acc[:, cols] = r
+
+        @pl.when(u > 0)
+        def _():
+            acc[:, cols] += r
+
+    def finish(k):
+        n = 3 * lane
+        for s in TWO:
+            cols = pl.ds(s * share + (k - 6) * n, n)
+            y_ref[:, cols] = (x1[:, cols].astype(F32) + acc[:, s * n:(s + 1) * n] + bdown[:, cols]).astype(BF)
+
     def run_down(k, lo=0, hi=UNITS, known=UNITS, primed=False):
-        order = lambda o: jnp.where(o == 2, 3, jnp.where(o == 3, 2, o))
-        n = 16 * (rows // 3)
-
-        def split(u):
-            c = lax.rem(u, 3)
-            _, _, i2 = place(c)
-            return c, wrap(i2 + order(u // 3))
-
         def load(u):
-            c, z = split(u)
+            c, z = quarter(u)
             load_rows(k, c, z, lax.rem(u, SLOTS))
         if not primed:
             load(lo)
@@ -449,23 +474,23 @@
             @pl.when(u + 2 < known)
             def _():
                 load(u + 2)
-            c, z = split(u)
-            at = pl.ds(pl.multiple_of((c * 4 + z) * n, lane), n)
-            r = jnp.dot(a[:, at], wbuf3[slot].reshape(n, 6 * lane), preferred_element_type=F32)
-
-            @pl.when(u == 0)
-            def _():
-                acc[...] = r
-
-            @pl.when(u > 0)
-            def _():
-                acc[...] += r
+            w = wbuf3[slot].reshape(-1, 6 * lane)
+            add(u, slice(None), jnp.dot(down_lhs(*quarter(u)), w, preferred_element_type=F32))
         loop(hi, step, lo)
         if hi == UNITS:
-            n = 3 * lane
-            for s in range(2):
-                cols = pl.ds(s * share + (k - 6) * n, n)
-                y_ref[:, cols] = (x1[:, cols].astype(F32) + acc[:, s * n:(s + 1) * n] + bdown[:, cols]).astype(BF)
+            finish(k)
+
+    def run_last(lo, hi):
+        n = 3 * lane
+
+        def step(u):
+            c, z = quarter(u)
+            for s in TWO:
+                w = G8[3 * s + c, z].reshape(-1, n)
+                add(u, slice(s * n, (s + 1) * n), jnp.dot(down_lhs(c, z), w, preferred_element_type=F32))
+        loop(hi, step, lo)
+        if hi == UNITS:
+            finish(LAST)
 
     def norm(src, which):
         n = seq // 8
@@ -486,7 +511,7 @@
             q_rows = pl.ds(pl.multiple_of(i * hd, hd), hd)
             k_rows = q_rows
             v_rows = pl.ds(pl.multiple_of(i * hd + d, hd), hd)
-            for b in range(2):
+            for b in TWO:
                 n = (b + 1) * qb
                 q = qt[q_rows, b * qb:n]
                 s = lax.dot_general(q, kv_ref[k_rows, :n], (((0,), (0,)), ((), ())),
@@ -554,35 +579,38 @@
     visit1(1)
     v_long(0, bqkv, d, 9)
     visit2(1)
-    run_units(load_cols, 0, qkv_unit(0), hi=QKV)
+    run_units(0, qkv_unit, hi=QKV)
     visit1(2)
     v_long(1, bup, 4 * d, 12)
     visit2(2)
-    run_units(load_cols, 1, qkv_unit(1), hi=QKV)
+    run_units(1, qkv_unit, hi=QKV)
     visit1(3)
     visit2(3)
-    run_units(load_cols, 2, qkv_unit(2), hi=QKV)
-    a1 = heads * 5 // UNITS
-    a2 = heads * QKV // UNITS
+    run_units(2, qkv_unit, hi=QKV)
+    q1, q2, q3 = 3, 6, QKV
+    a1, a2 = heads * q3 // 24, heads * 18 // 24
     attend(0, a1)
     visit1(4)
     attend(a1, a2)
     visit2(4)
     attend(a2, heads)
     flip()
-    for k in THREE:
-        run_units(load_cols, k, out_unit(k), QKV)
+    run_units(0, out_unit, QKV)
+    run_units(1, out_unit, QKV)
     visit1(5)
+    run_units(2, out_unit, QKV)
     norm(x1, 2)
-    run_units(load_cols, 3, up_unit(3))
+    run_units(3, up_unit, hi=q1, known=UNITS)
     visit2(5)
-    run_units(load_cols, 4, up_unit(4))
+    run_units(3, up_unit, q1, primed=True)
+    run_units(4, up_unit, hi=q2, known=UNITS)
     visit1(6)
+    run_units(4, up_unit, q2, primed=True)
     visit2(6)
-    run_units(load_cols, 5, up_unit(5))
+    run_units(5, up_unit, hi=q3, known=UNITS)
     visit1(7)
+    run_units(5, up_unit, q3, primed=True)
     visit2(7)
-    q1, q2, q3 = 3, 6, QKV
     run_down(6, hi=q2)
     sides_in(7)
     run_down(6, q2, primed=True)
@@ -593,15 +621,15 @@
     visit2(LAST)
     run_down(7, q3)
     await_siblings(LAST, 0)
-    run_down(LAST, hi=q1, known=q1)
+    run_last(0, q1)
     sides_in(LAST)
     await_siblings(LAST, SIDES[0])
-    run_down(LAST, q1, q2, q2)
+    run_last(q1, q2)
     across_in(LAST)
     await_siblings(LAST, SIDES[1])
-    run_down(LAST, q2, q3, q3)
+    run_last(q2, q3)
     await_siblings(LAST, ACROSS)
-    run_down(LAST, q3)
+    run_last(q3, UNITS)
 
     for k in range(CHUNKS):
         ref = Block(k).ref
@@ -609,9 +637,9 @@
             take(ref.at[(ALL3,) + ZEROS[:2 - p] + (ALL3,)], S.at[k, p])
         take(ref.at[ALL3], S.at[k, SIBLING])
     for m, lo, n in ((0,) + early, (0,) + rest, (1,) + whole):
-        take(stage12.at[m, pl.ds(0, 7), :, pl.ds(lo, n)], XS.at[2 * m + (lo > 0)])
+        take(stage12.at[m, OTHERS, :, pl.ds(lo, n)], XS.at[2 * m + (lo > 0)])
     take(stage3.at[0], XS.at[4])
-    take(V.at[0, 0, pl.ds(0, 7)], VS.at[0])
+    take(V.at[0, 0, OTHERS], VS.at[0])
     take(V.at[0, ALL3], VS.at[1])
     take(V.at[ALL3], VS.at[2])
 
@@ -647,7 +675,7 @@
                 pltpu.VMEM((seq, d), BF),
                 pltpu.VMEM((2 * d, seq), BF),
                 jax.ShapeDtypeStruct((36, 4, 4, 4, rows, lane), BF),
-                jax.ShapeDtypeStruct((18, 4, 4, 4, third, 3 * lane), BF),
+                jax.ShapeDtypeStruct((12, 4, 4, 4, third, 3 * lane), BF),
             ),
             in_specs=[hbm] + [vm] * 13,
             out_specs=(vm, vm, hbm, hbm),
@@ -659,6 +687,7 @@
                 pltpu.VMEM((seq, 6 * lane), F32),
                 pltpu.VMEM((18, rows, lane), BF),
                 pltpu.VMEM((9, third, 3 * lane), BF),
+                pltpu.VMEM((6, 4, 4, 4, third, 3 * lane), BF),
                 pltpu.VMEM((r, 4 * d), BF),
                 pltpu.VMEM((2, LINE, r, QKV * lane), BF),
                 pltpu.VMEM((2, w_down.shape[0], QKV * lane), BF),
@@ -681,7 +710,7 @@
                 dma((3,)),
             ],
             compiler_params=pltpu.CompilerParams(
-                has_side_effects=True, collective_id=0, vmem_limit_bytes=50 << 20),
+                has_side_effects=True, collective_id=0, vmem_limit_bytes=54 << 20),
             name="layer",
         )(prompts[0], w_qkv.reshape(r, -1), w_out, w_up, w_down, jnp.asarray(tab, jnp.int32), *(p[None] for p in parts))
         kc, vc = (m.reshape(heads, hd, seq).transpose(2, 0, 1)[None] for m in (kv[:d], kv[d:]))

time: 293 us -> 284 us (0.969)
  Pallas kernels: 286 us -> 277 us
    pallas_call x1, Pallas kernels: 286 us -> 277 us  [local_layer(): pl.pallas_call(functools.partial(layer_kernel, dims), out_shape=(pltpu.VM...]
where the time goes in v6:
time: 284 us
  Pallas kernels  277 us (98%)
  local copies, waits for them, and re-layouts  5.95 us (2%)
    pallas_call x1, Pallas kernels, local_layer(): pl.pallas_call(functools.partial(layer_kernel, dims), out_shape=(pltpu.VM...  277 us

profile of v6, /device:TPU:1, one launch (start us, length us, event | category | flops | bytes accessed | tf_op | source)
XLA Modules:
  0.0 283.5 jit_solution(16155899927489869092)
XLA Ops:
  0.6 2.1 reshape.15.wq
  2.7 276.9 %layer.1 = (bf16[512,2304]{1,0:T(8,128)(2,1)S(1)}, bf16[4608,512]{1,0:T(8,128)(2,1)S(1)}, bf16[36,4,4,4,144,128]{5,4,3,2,1,0:T(8,128)(2,1)}, bf16[12,4,4,4,48,384]{5,4,3,2,1,0:T(8,128)(2,1)}) custom-call(bf16[512,2304]{1,0:T(8,128)(2,1)} %bitcast.23, bf16[18,6912]{1,0:T(8,128)(2,1)} %reshape.15.wq, bf16[18,2304]{1,0:T(8,128)(2,1)} %wo.1, ...), custom_call_target="tpu_custom_call" | custom-call | tf_op jit(solution)/shard_map/layer/pallas_call | solution.py:672
  279.6 1.4 copy.18
  281.0 2.5 fusion

commit v7 on v6

--- a/solution.py
+++ b/solution.py
@@ -323,15 +323,13 @@
     def visit1(t):
         last, ahead, far = t - 1, t + 1, t + 2
         if t:
-            if t < LAST:
-                sides_in(last)
+            sides_in(last)
             across_in(last)
         if far < CHUNKS:
             p0_forward(far)
         if ahead < CHUNKS:
             axis_forward(ahead, 1)
-        if t < LAST:
-            axis_second(t, 2)
+        axis_second(t, 2)
 
     def visit2(t):
         last, ahead, far, farther = t - 1, t + 1, t + 2, t + 3
@@ -346,9 +344,7 @@
             issue(ahead)
         if ahead == LAST:
             axis_second(LAST, 2)
-        if t == LAST:
-            await_siblings(last, ACROSS)
-        elif t:
+        if t:
             await_siblings(last, *QUARTERS)
 
     def load_cols(k, u, slot):
@@ -480,17 +476,16 @@
         if hi == UNITS:
             finish(k)
 
-    def run_last(lo, hi):
+    def run_last(lo, hi, s, ahead=None):
         n = 3 * lane
+        cols = pl.ds(pl.multiple_of(s * n, lane), n)
 
         def step(u):
             c, z = quarter(u)
-            for s in TWO:
-                w = G8[3 * s + c, z].reshape(-1, n)
-                add(u, slice(s * n, (s + 1) * n), jnp.dot(down_lhs(c, z), w, preferred_element_type=F32))
+            if ahead is not None:
+                take(G8.at[c, ahead], R.at[LAST * 3 + c, SIBLING, ahead])
+            add(u, cols, jnp.dot(down_lhs(c, z), G8[3 * s + c, z].reshape(-1, n), preferred_element_type=F32))
         loop(hi, step, lo)
-        if hi == UNITS:
-            finish(LAST)
 
     def norm(src, which):
         n = seq // 8
@@ -614,22 +609,24 @@
     run_down(6, hi=q2)
     sides_in(7)
     run_down(6, q2, primed=True)
-    await_siblings(7, 0, *SIDES)
+    across_in(7)
+    await_siblings(7, FIRST, *SIDES)
     run_down(7, hi=q2, known=q3)
-    visit1(LAST)
+    axis_forward(LAST, 2)
     run_down(7, q2, q3, q3, True)
-    visit2(LAST)
+    await_siblings(7, ACROSS)
     run_down(7, q3)
-    await_siblings(LAST, 0)
-    run_last(0, q1)
+    other = 1 - core
     sides_in(LAST)
-    await_siblings(LAST, SIDES[0])
-    run_last(q1, q2)
+    run_last(FIRST, q1, core)
+    run_last(FIRST, q1, other, FIRST)
+    run_last(q1, q3, core)
+    run_last(q1, q2, other, SIDES[0])
     across_in(LAST)
-    await_siblings(LAST, SIDES[1])
-    run_last(q2, q3)
-    await_siblings(LAST, ACROSS)
-    run_last(q3, UNITS)
+    run_last(q2, q3, other, SIDES[1])
+    run_last(q3, UNITS, core)
+    run_last(q3, UNITS, other, ACROSS)
+    finish(LAST)
 
     for k in range(CHUNKS):
         ref = Block(k).ref

time: 284 us -> 281 us (0.989)
  Pallas kernels: 277 us -> 274 us
    pallas_call x1, Pallas kernels: 277 us -> 274 us  [local_layer(): pl.pallas_call(functools.partial(layer_kernel, dims), out_shape=(pltpu.VM...]
where the time goes in v7:
time: 281 us; the launch traced here: 280 us
  Pallas kernels  274 us (98%)
  local copies, waits for them, and re-layouts  5.95 us (2%)
    pallas_call x1, Pallas kernels, local_layer(): pl.pallas_call(functools.partial(layer_kernel, dims), out_shape=(pltpu.VM...  274 us

profile of v7, /device:TPU:1, one launch (start us, length us, event | category | flops | bytes accessed | tf_op | source)
XLA Modules:
  0.0 280.2 jit_solution(3129340798710613049)
XLA Ops:
  0.6 2.1 reshape.15.wq
  2.7 273.6 %layer.1 = (bf16[512,2304]{1,0:T(8,128)(2,1)S(1)}, bf16[4608,512]{1,0:T(8,128)(2,1)S(1)}, bf16[36,4,4,4,144,128]{5,4,3,2,1,0:T(8,128)(2,1)}, bf16[12,4,4,4,48,384]{5,4,3,2,1,0:T(8,128)(2,1)}) custom-call(bf16[512,2304]{1,0:T(8,128)(2,1)} %bitcast.23, bf16[18,6912]{1,0:T(8,128)(2,1)} %reshape.15.wq, bf16[18,2304]{1,0:T(8,128)(2,1)} %wo.1, ...), custom_call_target="tpu_custom_call" | custom-call | tf_op jit(solution)/shard_map/layer/pallas_call | solution.py:669
  276.3 1.4 copy.18
  277.7 2.5 fusion

commit v8 on v7

--- a/solution.py
+++ b/solution.py
@@ -545,6 +545,7 @@
         x_blocks(k)
         p0_send(k)
     p0_forward(0)
+    v_send(1)
     x3_blocks()
     await_group(0, 0, ACROSS)
     axis_first(0, 1)
@@ -556,13 +557,12 @@
     axis_first(1, 1)
     axis_second(1, 1)
     x_send(1, *whole)
-    v_send(1)
+    v_send(2)
     p0_send(7)
     p0_send(8)
     await_group(0, 1, SECOND)
     await_group(0, 1, ACROSS)
     axis_first(0, 2)
-    v_send(2)
     visit1(0)
     x_copy.wait()
     x_wait(1, *whole)
@@ -583,7 +583,7 @@
     visit2(3)
     run_units(2, qkv_unit, hi=QKV)
     q1, q2, q3 = 3, 6, QKV
-    a1, a2 = heads * q3 // 24, heads * 18 // 24
+    a1, a2 = heads * 7 // 24, heads * 14 // 24
     attend(0, a1)
     visit1(4)
     attend(a1, a2)
@@ -591,20 +591,19 @@
     attend(a2, heads)
     flip()
     run_units(0, out_unit, QKV)
+    visit1(5)
     run_units(1, out_unit, QKV)
-    visit1(5)
     run_units(2, out_unit, QKV)
+    visit2(5)
     norm(x1, 2)
-    run_units(3, up_unit, hi=q1, known=UNITS)
-    visit2(5)
-    run_units(3, up_unit, q1, primed=True)
+    run_units(3, up_unit)
+    visit1(6)
     run_units(4, up_unit, hi=q2, known=UNITS)
-    visit1(6)
+    visit2(6)
     run_units(4, up_unit, q2, primed=True)
-    visit2(6)
-    run_units(5, up_unit, hi=q3, known=UNITS)
+    run_units(5, up_unit, hi=q2, known=UNITS)
     visit1(7)
-    run_units(5, up_unit, q3, primed=True)
+    run_units(5, up_unit, q2, primed=True)
     visit2(7)
     run_down(6, hi=q2)
     sides_in(7)

time: 281 us -> 275 us (0.979)
  Pallas kernels: 274 us -> 268 us
    pallas_call x1, Pallas kernels: 274 us -> 268 us  [local_layer(): pl.pallas_call(functools.partial(layer_kernel, dims), out_shape=(pltpu.VM...]
where the time goes in v8:
time: 275 us; the launch traced here: 274 us
  Pallas kernels  268 us (97%)
  local copies, waits for them, and re-layouts  5.95 us (2%)
    pallas_call x1, Pallas kernels, local_layer(): pl.pallas_call(functools.partial(layer_kernel, dims), out_shape=(pltpu.VM...  268 us

profile of v8, /device:TPU:1, one launch (start us, length us, event | category | flops | bytes accessed | tf_op | source)
XLA Modules:
  0.0 274.3 jit_solution(9541695568507082862)
XLA Ops:
  0.6 2.1 reshape.15.wq
  2.7 267.7 %layer.1 = (bf16[512,2304]{1,0:T(8,128)(2,1)S(1)}, bf16[4608,512]{1,0:T(8,128)(2,1)S(1)}, bf16[36,4,4,4,144,128]{5,4,3,2,1,0:T(8,128)(2,1)}, bf16[12,4,4,4,48,384]{5,4,3,2,1,0:T(8,128)(2,1)}) custom-call(bf16[512,2304]{1,0:T(8,128)(2,1)} %bitcast.23, bf16[18,6912]{1,0:T(8,128)(2,1)} %reshape.15.wq, bf16[18,2304]{1,0:T(8,128)(2,1)} %wo.1, ...), custom_call_target="tpu_custom_call" | custom-call | tf_op jit(solution)/shard_map/layer/pallas_call | solution.py:668
  270.4 1.4 copy.18
  271.9 2.5 fusion
